TPU v7x, 8 devices: a whole 2x2x1 slice. The times are simulated.
8 devices in a mesh: dp: 2 (over z, y), tp: 4 (over x, core).
Axes of the slice: x: 2, y: 2, z: 1, core: 2. Of those that a mesh axis runs over, the one named last changes fastest.
Arguments:
- y_one: float32 [8, 32, 2048], P('dp'), parts along dimension 0
- y_two: float32 [8, 32, 2048], P('dp'), parts along dimension 0
- dy_one: float32 [8, 32, 2048], P('dp'), parts along dimension 0
- dy_two: float32 [8, 32, 2048], P('dp'), parts along dimension 0
- seq_lens: int32 [8], P('dp'), parts along dimension 0
- w_query: bfloat16 [3, 2048, 32, 64], P(None, None, 'tp')
- w_key: bfloat16 [3, 2048, 8, 64], P(None, None, 'tp')
- w_value: bfloat16 [3, 2048, 8, 64], P(None, None, 'tp')
- w_out: bfloat16 [3, 32, 64, 2048], P(None, 'tp')
- w_up: bfloat16 [3, 2048, 8192], P(None, None, 'tp')
- w_down: bfloat16 [3, 8192, 2048], P(None, 'tp')
Outputs:
- output 1: float32 [8, 32, 2048], P('dp'), parts along dimension 0
- output 2: float32 [8, 32, 2048], P('dp'), parts along dimension 0
- output 3: float32 [8, 32, 2048], P('dp'), parts along dimension 0
- output 4: float32 [8, 32, 2048], P('dp'), parts along dimension 0
- output 5: float32 [6, 2048, 32, 64], P('dp', None, 'tp'), parts along dimension 0
- output 6: float32 [6, 2048, 8, 64], P('dp', None, 'tp'), parts along dimension 0
- output 7: float32 [6, 2048, 8, 64], P('dp', None, 'tp'), parts along dimension 0
- output 8: float32 [6, 32, 64, 2048], P('dp', 'tp'), parts along dimension 0
- output 9: float32 [6, 2048, 8192], P('dp', None, 'tp'), parts along dimension 0
- output 10: float32 [6, 8192, 2048], P('dp', 'tp'), parts along dimension 0
There are 2 independent parts. A program takes and returns all parts, laid end to end along the dimension named above; an argument that names none is the same for every part.
All inputs are finite; a program needn't handle non-finite values.
Results may differ from a plain program's by a relative error of at most 0.02.
Values are sent between devices in bfloat16 or wider.
A program may use at most 1 GiB of HBM per device.

v0:
```python
import jax
import jax.numpy as jnp
from jax import lax
from jax.sharding import PartitionSpec as P, NamedSharding

F32 = jnp.float32
BF16 = jnp.bfloat16
EPS = 1e-5
MASK_VALUE = -1e30


def rms_norm(x_val):
    inv_rms = lax.rsqrt(jnp.mean(x_val * x_val, axis=-1, keepdims=True) + EPS)
    return x_val * inv_rms, inv_rms


def rms_back(normed, inv_rms, grad_norm):
    return inv_rms * (grad_norm - normed * jnp.mean(grad_norm * normed, axis=-1, keepdims=True))


def visible_mask(seq_lens, seq_len):
    row_pos = lax.broadcasted_iota(jnp.int32, (seq_len, seq_len), 0)
    col_pos = lax.broadcasted_iota(jnp.int32, (seq_len, seq_len), 1)
    causal = (col_pos <= row_pos)[None, None, None]
    in_length = col_pos[None, None, None] < seq_lens[:, None, None, None, None]
    return causal & in_length


def block_back(carry, seq_lens, layer_w, all_reduce):
    y_one, y_two, dy_one, dy_two = carry
    w_query, w_key, w_value, w_out, w_up, w_down = layer_w
    n_batch, seq_len = y_one.shape[0], y_one.shape[1]
    n_heads, head_dim = w_query.shape[1], w_query.shape[2]
    kv_slots = w_key.shape[1]
    group_size = n_heads // kv_slots
    score_scale = head_dim ** -0.5

    norm_g, inv_g = rms_norm(y_one)
    norm_g_b = norm_g.astype(BF16)
    pre_act = jnp.einsum('bsd,df->bsf', norm_g_b, w_up, preferred_element_type=F32)
    act_val, gelu_back = jax.vjp(jax.nn.gelu, pre_act)
    act_b = act_val.astype(BF16)
    x_two = y_two - all_reduce(jnp.einsum('bsf,fd->bsd', act_b, w_down, preferred_element_type=F32))
    dy2_b = dy_two.astype(BF16)
    d_act = jnp.einsum('bsd,fd->bsf', dy2_b, w_down, preferred_element_type=F32)
    d_pre = gelu_back(d_act)[0].astype(BF16)
    dw_down = jnp.einsum('bsf,bsd->fd', act_b, dy2_b, preferred_element_type=F32)
    dw_up = jnp.einsum('bsd,bsf->df', norm_g_b, d_pre, preferred_element_type=F32)
    grad_norm_g = all_reduce(jnp.einsum('bsf,df->bsd', d_pre, w_up, preferred_element_type=F32))
    dy_one = dy_one + rms_back(norm_g, inv_g, grad_norm_g)

    norm_f, inv_f = rms_norm(x_two)
    norm_f_b = norm_f.astype(BF16)
    query_proj = jnp.einsum('bsd,dhe->bshe', norm_f_b, w_query, preferred_element_type=F32).astype(BF16)
    query_grp = query_proj.reshape(n_batch, seq_len, kv_slots, group_size, head_dim)
    key_proj = jnp.einsum('bsd,dge->bsge', norm_f_b, w_key, preferred_element_type=F32).astype(BF16)
    value_proj = jnp.einsum('bsd,dge->bsge', norm_f_b, w_value, preferred_element_type=F32).astype(BF16)
    scores = jnp.einsum('bigre,bjge->bgrij', query_grp, key_proj, preferred_element_type=F32) * score_scale
    scores = jnp.where(visible_mask(seq_lens, seq_len), scores, MASK_VALUE)
    attn_probs = jax.nn.softmax(scores, axis=-1)
    probs_b = attn_probs.astype(BF16)
    attn_out = jnp.einsum('bgrij,bjge->bigre', probs_b, value_proj, preferred_element_type=F32).astype(BF16)
    attn_out = attn_out.reshape(n_batch, seq_len, n_heads, head_dim)
    x_one = y_one - all_reduce(jnp.einsum('bihe,hed->bid', attn_out, w_out, preferred_element_type=F32))
    dy1_b = dy_one.astype(BF16)
    dw_out = jnp.einsum('bihe,bid->hed', attn_out, dy1_b, preferred_element_type=F32)
    d_attn = jnp.einsum('bid,hed->bihe', dy1_b, w_out, preferred_element_type=F32).astype(BF16)
    d_attn = d_attn.reshape(n_batch, seq_len, kv_slots, group_size, head_dim)
    d_value = jnp.einsum('bgrij,bigre->bjge', probs_b, d_attn, preferred_element_type=F32).astype(BF16)
    d_probs = jnp.einsum('bigre,bjge->bgrij', d_attn, value_proj, preferred_element_type=F32)
    d_scores = (attn_probs * (d_probs - jnp.sum(d_probs * attn_probs, axis=-1, keepdims=True)) * score_scale).astype(BF16)
    d_query = jnp.einsum('bgrij,bjge->bigre', d_scores, key_proj, preferred_element_type=F32).astype(BF16)
    d_query = d_query.reshape(n_batch, seq_len, n_heads, head_dim)
    d_key = jnp.einsum('bgrij,bigre->bjge', d_scores, query_grp, preferred_element_type=F32).astype(BF16)
    dw_query = jnp.einsum('bsd,bshe->dhe', norm_f_b, d_query, preferred_element_type=F32)
    dw_key = jnp.einsum('bsd,bsge->dge', norm_f_b, d_key, preferred_element_type=F32)
    dw_value = jnp.einsum('bsd,bsge->dge', norm_f_b, d_value, preferred_element_type=F32)
    grad_norm_f = all_reduce(jnp.einsum('bshe,dhe->bsd', d_query, w_query, preferred_element_type=F32)
                             + jnp.einsum('bsge,dge->bsd', d_key, w_key, preferred_element_type=F32)
                             + jnp.einsum('bsge,dge->bsd', d_value, w_value, preferred_element_type=F32))
    dx_two = dy_two + rms_back(norm_f, inv_f, grad_norm_f)
    return (x_one, x_two, dy_one, dx_two), (dw_query, dw_key, dw_value, dw_out, dw_up, dw_down)


def stack_grads(grads_by_layer):
    return tuple(jnp.stack([layer_grads[grad_pos] for layer_grads in grads_by_layer]) for grad_pos in range(6))


def tp_sum(partial_val):
    return lax.psum(partial_val, 'tp')


def solution(mesh):
    act_spec = P('dp', None, None)
    w_specs = (P(None, None, 'tp', None), P(None, None, 'tp', None), P(None, None, 'tp', None),
               P(None, 'tp', None, None), P(None, None, 'tp'), P(None, 'tp', None))
    g_specs = (P('dp', None, 'tp', None), P('dp', None, 'tp', None), P('dp', None, 'tp', None),
               P('dp', 'tp', None, None), P('dp', None, 'tp'), P('dp', 'tp', None))

    def local_fn(y_one, y_two, dy_one, dy_two, seq_lens, w_query, w_key, w_value, w_out, w_up, w_down):
        weights = (w_query, w_key, w_value, w_out, w_up, w_down)
        carry = (y_one, y_two, dy_one, dy_two)
        n_layers = w_query.shape[0]
        grads_by_layer = [None] * n_layers
        for layer_idx in reversed(range(n_layers)):
            layer_w = tuple(w_stack[layer_idx] for w_stack in weights)
            carry, grads_by_layer[layer_idx] = block_back(carry, seq_lens, layer_w, tp_sum)
        return carry + stack_grads(grads_by_layer)

    return jax.shard_map(local_fn, mesh=mesh,
                         in_specs=(act_spec,) * 4 + (P('dp'),) + w_specs,
                         out_specs=(act_spec,) * 4 + g_specs,
                         check_vma=False)
```

profile of v0, /device:TPU:0, one launch (start us, length us, event | category | flops | bytes accessed | tf_op | source)
XLA Modules:
  0.0 524.5 jit_solution(16843879995199308229)
XLA Ops:
  8.6 5.0 fusion.28
  13.7 5.9 %fusion.24 = f32[4,32,2048]{2,1,0:T(8,128)} fusion(bf16[3,2048,2048]{2,1,0:T(8,128)(2,1)} %param.21, f32[4,32,2048]{2,1,0:T(8,128)S(1)} %fusion.28), kind=kOutput, calls=%fused_computation.34 | convolution fusion | flops 1076101120 | bytes 10485760 | tf_op jit(solution)/shard_map/bsf,fd->bsd/dot_general | solution.py:43
  19.5 6.6 %fusion.144 = bf16[4,32,2048]{2,1,0:T(8,128)(2,1)S(1)} fusion(f32[4,32,2048]{2,1,0:T(8,128)S(1)} %fusion.28, bf16[3,2048,2048]{2,1,0:T(8,128)(2,1)} %param.21, f32[4,32,2048]{2,1,0:T(8,128)S(1)} %copy-done.20), kind=kOutput, calls=%fused_computation.198 | convolution fusion | flops 1079246848 | bytes 11010048 | tf_op jit(solution)/shard_map/bsd,fd->bsf/dot_general | solution.py:45
  26.9 7.3 %fusion.26 = f32[4,32,2048]{2,1,0:T(8,128)} fusion(bf16[4,32,2048]{2,1,0:T(8,128)(2,1)S(1)} %fusion.144, bf16[3,2048,2048]{2,1,0:T(8,128)(2,1)} %param.20), kind=kOutput, calls=%fused_computation.36 | convolution fusion | flops 1073741824 | bytes 9961472 | tf_op jit(solution)/shard_map/bsf,df->bsd/dot_general | solution.py:49
  34.5 9.7 %convolution_bitcast_fusion.3 = f32[1,2048,2048]{2,1,0:T(8,128)} fusion(bf16[4,32,2048]{2,1,0:T(8,128)(2,1)} %copy-done.34, f32[4,32,2048]{2,1,0:T(8,128)S(1)} %copy-done.2, f32[4,32]{1,0:T(4,128)S(1)} %add_rsqrt_fusion.5), kind=kOutput, calls=%fused_computation.13 | convolution fusion | flops 1074266112 | bytes 18350592 | tf_op jit(solution)/shard_map/bsd,bsf->df/dot_general | solution.py:48
  44.3 8.1 %convolution_bitcast_fusion = f32[1,2048,2048]{2,1,0:T(8,128)} fusion(f32[4,32,2048]{2,1,0:T(8,128)S(1)} %copy-done.20, f32[4,32,2048]{2,1,0:T(8,128)S(1)} %fusion.28), kind=kOutput, calls=%fused_computation.10 | convolution fusion | flops 1076363264 | bytes 18874368 | tf_op jit(solution)/shard_map/bsf,bsd->fd/dot_general | solution.py:47
  52.4 30.5 %all-reduce.23.cloned.1.call-done = (f32[4,32,2048]{2,1,0:T(8,128)}, f32[4,32,2048]{2,1,0:T(8,128)}) async-done(((f32[4,32,2048]{2,1,0:T(8,128)}, f32[4,32,2048]{2,1,0:T(8,128)}), (f32[4,32,2048]{2,1,0:T(8,128)}, f32[4,32,2048]{2,1,0:T(8,128)})) %all-reduce.23.cloned.1.call-update) | async-done | bytes 2097168 | tf_op jit(solution)/shard_map/psum | solution.py:90
  84.4 2.5 multiply_reduce_fusion.10
  87.1 3.0 fusion.102
  93.1 2.8 fusion.105
  108.7 3.1 convolution_bitcast_fusion.29
  111.8 3.1 fusion.43
  118.1 2.8 convolution_bitcast_fusion.6
  120.9 2.7 convolution_bitcast_fusion.9
  123.6 37.2 %all-reduce.21.cloned.1.call-done = (f32[4,32,2048]{2,1,0:T(8,128)}, f32[4,32,2048]{2,1,0:T(8,128)}) async-done(((f32[4,32,2048]{2,1,0:T(8,128)}, f32[4,32,2048]{2,1,0:T(8,128)}), (f32[4,32,2048]{2,1,0:T(8,128)}, f32[4,32,2048]{2,1,0:T(8,128)})) %all-reduce.21.cloned.1.call-update) | async-done | bytes 2097168 | tf_op jit(solution)/shard_map/psum | solution.py:90
  164.5 4.8 fusion.20
  169.3 6.1 %fusion.16 = f32[4,32,2048]{2,1,0:T(8,128)} fusion(bf16[3,2048,2048]{2,1,0:T(8,128)(2,1)} %param.21, f32[4,32,2048]{2,1,0:T(8,128)S(1)} %fusion.20), kind=kOutput, calls=%fused_computation.26 | convolution fusion | flops 1076101120 | bytes 10485760 | tf_op jit(solution)/shard_map/bsf,fd->bsd/dot_general | solution.py:43
  175.4 6.6 %fusion.151 = bf16[4,32,2048]{2,1,0:T(8,128)(2,1)S(1)} fusion(f32[4,32,2048]{2,1,0:T(8,128)S(1)} %fusion.20, bf16[3,2048,2048]{2,1,0:T(8,128)(2,1)} %param.21, f32[4,32,2048]{2,1,0:T(8,128)S(1)} %multiply_add_fusion.4), kind=kOutput, calls=%fused_computation.205 | convolution fusion | flops 1079246848 | bytes 11010048 | tf_op jit(solution)/shard_map/bsd,fd->bsf/dot_general | solution.py:45
  182.8 7.2 %fusion.18 = f32[4,32,2048]{2,1,0:T(8,128)} fusion(bf16[4,32,2048]{2,1,0:T(8,128)(2,1)S(1)} %fusion.151, bf16[3,2048,2048]{2,1,0:T(8,128)(2,1)} %param.20), kind=kOutput, calls=%fused_computation.28 | convolution fusion | flops 1073741824 | bytes 9961472 | tf_op jit(solution)/shard_map/bsf,df->bsd/dot_general | solution.py:49
  190.3 9.3 %convolution_bitcast_fusion.4 = f32[1,2048,2048]{2,1,0:T(8,128)} fusion(bf16[4,32,2048]{2,1,0:T(8,128)(2,1)} %copy-done.35, f32[4,32,2048]{2,1,0:T(8,128)S(1)} %get-tuple-element.29, f32[4,32]{1,0:T(4,128)S(1)} %add_rsqrt_fusion.3), kind=kOutput, calls=%fused_computation.14 | convolution fusion | flops 1074266112 | bytes 18350592 | tf_op jit(solution)/shard_map/bsd,bsf->df/dot_general | solution.py:48
  199.6 8.1 %convolution_bitcast_fusion.1 = f32[1,2048,2048]{2,1,0:T(8,128)} fusion(f32[4,32,2048]{2,1,0:T(8,128)S(1)} %copy-done.11, f32[4,32,2048]{2,1,0:T(8,128)S(1)} %copy-done.32), kind=kOutput, calls=%fused_computation.11 | convolution fusion | flops 1076363264 | bytes 18874368 | tf_op jit(solution)/shard_map/bsf,bsd->fd/dot_general | solution.py:47
  207.8 28.2 %all-reduce.19.cloned.1.call-done = (f32[4,32,2048]{2,1,0:T(8,128)}, f32[4,32,2048]{2,1,0:T(8,128)}) async-done(((f32[4,32,2048]{2,1,0:T(8,128)}, f32[4,32,2048]{2,1,0:T(8,128)}), (f32[4,32,2048]{2,1,0:T(8,128)}, f32[4,32,2048]{2,1,0:T(8,128)})) %all-reduce.19.cloned.1.call-update) | async-done | bytes 2097168 | tf_op jit(solution)/shard_map/psum | solution.py:90
  239.2 2.7 fusion.108
  245.1 2.8 fusion.111
  260.7 3.1 convolution_bitcast_fusion.28
  263.8 3.1 fusion.45
  269.8 2.7 convolution_bitcast_fusion.7
  272.5 2.7 convolution_bitcast_fusion.10
  275.2 37.7 %all-reduce.17.cloned.1.call-done = (f32[4,32,2048]{2,1,0:T(8,128)}, f32[4,32,2048]{2,1,0:T(8,128)}) async-done(((f32[4,32,2048]{2,1,0:T(8,128)}, f32[4,32,2048]{2,1,0:T(8,128)}), (f32[4,32,2048]{2,1,0:T(8,128)}, f32[4,32,2048]{2,1,0:T(8,128)})) %all-reduce.17.cloned.1.call-update) | async-done | bytes 2097168 | tf_op jit(solution)/shard_map/psum | solution.py:90
  316.2 4.8 fusion.12
  321.0 6.6 %fusion.158 = bf16[4,32,2048]{2,1,0:T(8,128)(2,1)S(1)} fusion(f32[4,32,2048]{2,1,0:T(8,128)S(1)} %fusion.12, bf16[3,2048,2048]{2,1,0:T(8,128)(2,1)} %param.21, f32[4,32,2048]{2,1,0:T(8,128)S(1)} %multiply_add_fusion.2), kind=kOutput, calls=%fused_computation.212 | convolution fusion | flops 1079246848 | bytes 11010048 | tf_op jit(solution)/shard_map/bsd,fd->bsf/dot_general | solution.py:45
  327.6 8.1 %convolution_bitcast_fusion.2 = f32[1,2048,2048]{2,1,0:T(8,128)} fusion(f32[4,32,2048]{2,1,0:T(8,128)S(1)} %multiply_add_fusion.2, f32[4,32,2048]{2,1,0:T(8,128)S(1)} %fusion.12), kind=kOutput, calls=%fused_computation.12 | convolution fusion | flops 1076363264 | bytes 18874368 | tf_op jit(solution)/shard_map/bsf,bsd->fd/dot_general | solution.py:47
  335.7 8.2 %convolution_bitcast_fusion.5 = f32[1,2048,2048]{2,1,0:T(8,128)} fusion(bf16[4,32,2048]{2,1,0:T(8,128)(2,1)S(1)} %fusion.158, f32[4,32,2048]{2,1,0:T(8,128)S(1)} %get-tuple-element.25, f32[4,32]{1,0:T(4,128)S(1)} %add_rsqrt_fusion.1), kind=kOutput, calls=%fused_computation.15 | convolution fusion | flops 1074266112 | bytes 18350592 | tf_op jit(solution)/shard_map/bsd,bsf->df/dot_general | solution.py:48
  344.0 7.5 %fusion.10 = f32[4,32,2048]{2,1,0:T(8,128)} fusion(bf16[4,32,2048]{2,1,0:T(8,128)(2,1)S(1)} %fusion.158, bf16[3,2048,2048]{2,1,0:T(8,128)(2,1)} %param.20), kind=kOutput, calls=%fused_computation.20 | convolution fusion | flops 1073741824 | bytes 9961472 | tf_op jit(solution)/shard_map/bsf,df->bsd/dot_general | solution.py:49
  351.4 5.8 %fusion.8 = f32[4,32,2048]{2,1,0:T(8,128)} fusion(bf16[3,2048,2048]{2,1,0:T(8,128)(2,1)} %param.21, f32[4,32,2048]{2,1,0:T(8,128)S(1)} %fusion.12), kind=kOutput, calls=%fused_computation.18 | convolution fusion | flops 1076101120 | bytes 10485760 | tf_op jit(solution)/shard_map/bsf,fd->bsd/dot_general | solution.py:43
  357.3 35.7 %pad_maximum_fusion = f32[3,2048,2048]{2,1,0:T(8,128)} fusion(f32[1,2048,2048]{2,1,0:T(8,128)} %convolution_bitcast_fusion.3, f32[1,2048,2048]{2,1,0:T(8,128)} %convolution_bitcast_fusion.4, f32[1,2048,2048]{2,1,0:T(8,128)} %convolution_bitcast_fusion.5), kind=kLoop, calls=%fused_computation.6 | loop fusion | flops 25165824 | bytes 100663296 | tf_op jit(solution)/shard_map/stack | solution.py:86
  392.9 35.6 %pad_maximum_fusion.1 = f32[3,2048,2048]{2,1,0:T(8,128)} fusion(f32[1,2048,2048]{2,1,0:T(8,128)} %convolution_bitcast_fusion, f32[1,2048,2048]{2,1,0:T(8,128)} %convolution_bitcast_fusion.1, f32[1,2048,2048]{2,1,0:T(8,128)} %convolution_bitcast_fusion.2), kind=kLoop, calls=%fused_computation.7 | loop fusion | flops 25165824 | bytes 100663296 | tf_op jit(solution)/shard_map/stack | solution.py:86
  430.3 3.0 fusion.114
  437.9 2.8 fusion.117
  454.2 2.7 convolution_bitcast_fusion.11
  456.9 3.1 convolution_bitcast_fusion.27
  459.9 2.7 convolution_bitcast_fusion.8
  462.6 3.2 fusion.47
  465.8 4.0 pad_maximum_fusion.5
  471.8 11.8 %pad_maximum_fusion.3 = f32[3,8,64,2048]{3,2,1,0:T(8,128)} fusion(f32[1,8,64,2048]{3,2,1,0:T(8,128)} %convolution_bitcast_fusion.9, f32[1,8,64,2048]{3,2,1,0:T(8,128)} %convolution_bitcast_fusion.10, f32[1,8,64,2048]{3,2,1,0:T(8,128)} %convolution_bitcast_fusion.11), kind=kLoop, calls=%fused_computation.9 | loop fusion | flops 6291456 | bytes 25165824 | tf_op jit(solution)/shard_map/stack | solution.py:86
  483.5 10.1 %pad_maximum_fusion.2 = f32[3,2048,8,64]{1,3,2,0:T(8,128)} fusion(f32[1,2048,8,64]{1,3,2,0:T(8,128)S(1)} %copy-done, f32[1,2048,8,64]{1,3,2,0:T(8,128)} %convolution_bitcast_fusion.7, f32[1,2048,8,64]{1,3,2,0:T(8,128)} %convolution_bitcast_fusion.8), kind=kLoop, calls=%fused_computation.8 | loop fusion | flops 6291456 | bytes 25165824 | tf_op jit(solution)/shard_map/stack | solution.py:86
  493.6 18.2 %all-reduce.13.cloned.1.call-done = (f32[4,32,2048]{2,1,0:T(8,128)}, f32[4,32,2048]{2,1,0:T(8,128)}) async-done(((f32[4,32,2048]{2,1,0:T(8,128)}, f32[4,32,2048]{2,1,0:T(8,128)}), (f32[4,32,2048]{2,1,0:T(8,128)}, f32[4,32,2048]{2,1,0:T(8,128)})) %all-reduce.13.cloned.1.call-update) | async-done | bytes 2097168 | tf_op jit(solution)/shard_map/psum | solution.py:90
  513.3 2.8 multiply_add_fusion
  (155 shorter events, 77.5 us)
Async XLA Ops:
  7.2 75.7 %all-reduce.23.cloned.1.call-start = ((), (), s32[]{:S(2)}) async-start(), calls=%async_computation.5 | async-start | bytes 4194304 | tf_op jit(solution)/shard_map/psum | solution.py:90
  13.6 5.9 %copy-start.20 = (f32[4,32,2048]{2,1,0:T(8,128)S(1)}, f32[4,32,2048]{2,1,0:T(8,128)}, u32[]{:S(2)}) copy-start(f32[4,32,2048]{2,1,0:T(8,128)} %param.14) | copy-start | bytes 3145732
  26.1 0.8 copy-start.34
  26.9 7.6 %copy-start.2 = (f32[4,32,2048]{2,1,0:T(8,128)S(1)}, f32[4,32,2048]{2,1,0:T(8,128)}, u32[]{:S(2)}) copy-start(f32[4,32,2048]{2,1,0:T(8,128)} %param.11) | copy-start | bytes 3145732
  34.3 9.9 %copy-start.26 = (s32[4]{0:T(128)S(1)}, s32[4]{0:T(128)}, u32[]{:S(2)}) copy-start(s32[4]{0:T(128)} %param.15) | copy-start | bytes 52
  34.3 126.6 %all-reduce.21.cloned.1.call-start = ((), (), s32[]{:S(2)}) async-start(), calls=%async_computation.4 | async-start | bytes 4194304 | tf_op jit(solution)/shard_map/psum | solution.py:90
  44.3 397.8 %copy-start.25 = (pred[4,32,32]{1,2,0:T(8,128)(4,1)}, pred[4,32,32]{1,2,0:T(8,128)(4,1)S(1)}, u32[]{:S(2)}) copy-start(pred[4,32,32]{1,2,0:T(8,128)(4,1)S(1)} %fusion.234) | copy-start | bytes 12292
  86.9 34.0 %copy-start.7 = (f32[4,32,2048]{2,1,0:T(8,128)}, f32[4,32,2048]{2,1,0:T(8,128)S(1)}, u32[]{:S(2)}) copy-start(f32[4,32,2048]{2,1,0:T(8,128)S(1)} %get-tuple-element.38) | copy-start | bytes 3145732
  90.1 8.5 %copy-start.29 = (bf16[4,32,8,64]{3,1,2,0:T(8,128)(2,1)}, bf16[4,32,8,64]{3,1,2,0:T(8,128)(2,1)S(1)}, u32[]{:S(2)}) copy-start(bf16[4,32,8,64]{3,1,2,0:T(8,128)(2,1)S(1)} %fusion.102) | copy-start | bytes 393220
  114.9 121.1 %all-reduce.19.cloned.1.call-start = ((), (), s32[]{:S(2)}) async-start(), calls=%async_computation.3 | async-start | bytes 4194304 | tf_op jit(solution)/shard_map/psum | solution.py:90
  120.9 43.3 %copy-start.3 = (f32[4,32,2048]{2,1,0:T(8,128)S(1)}, f32[4,32,2048]{2,1,0:T(8,128)}, u32[]{:S(2)}) copy-start(f32[4,32,2048]{2,1,0:T(8,128)} %param.11) | copy-start | bytes 3145732
  160.8 3.4 copy-start.23
  164.2 11.2 %copy-start.10 = (f32[4,32,2048]{2,1,0:T(8,128)}, f32[4,32,2048]{2,1,0:T(8,128)S(1)}, u32[]{:S(2)}) copy-start(f32[4,32,2048]{2,1,0:T(8,128)S(1)} %multiply_add_fusion.4) | copy-start | bytes 3145732
  169.3 6.2 %copy-start.31 = (f32[4,32,2048]{2,1,0:T(8,128)}, f32[4,32,2048]{2,1,0:T(8,128)S(1)}, u32[]{:S(2)}) copy-start(f32[4,32,2048]{2,1,0:T(8,128)S(1)} %fusion.20) | copy-start | bytes 3145732
  182.0 0.8 copy-start.35
  190.1 9.5 %copy-start.11 = (f32[4,32,2048]{2,1,0:T(8,128)S(1)}, f32[4,32,2048]{2,1,0:T(8,128)}, u32[]{:S(2)}) copy-start(f32[4,32,2048]{2,1,0:T(8,128)} %copy-done.10) | copy-start | bytes 3145732
  190.1 122.8 %all-reduce.17.cloned.1.call-start = ((), (), s32[]{:S(2)}) async-start(), calls=%async_computation.2 | async-start | bytes 4194304 | tf_op jit(solution)/shard_map/psum | solution.py:90
  190.3 9.3 %copy-start.32 = (f32[4,32,2048]{2,1,0:T(8,128)S(1)}, f32[4,32,2048]{2,1,0:T(8,128)}, u32[]{:S(2)}) copy-start(f32[4,32,2048]{2,1,0:T(8,128)} %copy-done.31) | copy-start | bytes 3145732
  236.0 7.5 %copy-start.14 = (f32[4,32,2048]{2,1,0:T(8,128)S(1)}, f32[4,32,2048]{2,1,0:T(8,128)}, u32[]{:S(2)}) copy-start(f32[4,32,2048]{2,1,0:T(8,128)} %get-tuple-element.17) | copy-start | bytes 3145732
  236.0 7.8 %copy-start.8 = (f32[4,32,2048]{2,1,0:T(8,128)S(1)}, f32[4,32,2048]{2,1,0:T(8,128)}, u32[]{:S(2)}) copy-start(f32[4,32,2048]{2,1,0:T(8,128)} %copy-done.7) | copy-start | bytes 3145732
  241.9 8.6 %copy-start.27 = (bf16[4,32,8,64]{3,1,2,0:T(8,128)(2,1)}, bf16[4,32,8,64]{3,1,2,0:T(8,128)(2,1)S(1)}, u32[]{:S(2)}) copy-start(bf16[4,32,8,64]{3,1,2,0:T(8,128)(2,1)S(1)} %fusion.108) | copy-start | bytes 393220
  244.1 1.0 copy-start.4
  266.9 161.6 %all-reduce.15.cloned.1.call-start = ((), (), s32[]{:S(2)}) async-start(), calls=%async_computation.1 | async-start | bytes 4194304 | tf_op jit(solution)/shard_map/psum | solution.py:90
  267.2 5.3 %copy-start.5 = (f32[4,32,2048]{2,1,0:T(8,128)S(1)}, f32[4,32,2048]{2,1,0:T(8,128)}, u32[]{:S(2)}) copy-start(f32[4,32,2048]{2,1,0:T(8,128)} %copy-done.4) | copy-start | bytes 3145732
  272.5 41.9 %copy-start.12 = (f32[4,32,2048]{2,1,0:T(8,128)S(1)}, f32[4,32,2048]{2,1,0:T(8,128)}, u32[]{:S(2)}) copy-start(f32[4,32,2048]{2,1,0:T(8,128)} %copy-done.10) | copy-start | bytes 3145732
  312.9 3.1 copy-start.22
  316.0 11.7 %copy-start.9 = (f32[4,32,2048]{2,1,0:T(8,128)}, f32[4,32,2048]{2,1,0:T(8,128)S(1)}, u32[]{:S(2)}) copy-start(f32[4,32,2048]{2,1,0:T(8,128)S(1)} %multiply_add_fusion.2) | copy-start | bytes 3145732
  357.2 154.5 %all-reduce.13.cloned.1.call-start = ((), (), s32[]{:S(2)}) async-start(), calls=%async_computation | async-start | bytes 4194304 | tf_op jit(solution)/shard_map/psum | solution.py:90
  428.6 7.8 %copy-start.13 = (f32[4,32,2048]{2,1,0:T(8,128)S(1)}, f32[4,32,2048]{2,1,0:T(8,128)}, u32[]{:S(2)}) copy-start(f32[4,32,2048]{2,1,0:T(8,128)} %get-tuple-element.13) | copy-start | bytes 3145732
  428.6 8.1 %copy-start.6 = (f32[4,32,2048]{2,1,0:T(8,128)S(1)}, f32[4,32,2048]{2,1,0:T(8,128)}, u32[]{:S(2)}) copy-start(f32[4,32,2048]{2,1,0:T(8,128)} %copy-done.4) | copy-start | bytes 3145732
  430.1 83.2 %copy-start.1 = (f32[4,32,2048]{2,1,0:T(8,128)}, f32[4,32,2048]{2,1,0:T(8,128)S(1)}, u32[]{:S(2)}) copy-start(f32[4,32,2048]{2,1,0:T(8,128)S(1)} %get-tuple-element.23) | copy-start | bytes 3145732
  433.3 10.2 %copy-start.28 = (bf16[4,32,8,64]{3,1,2,0:T(8,128)(2,1)}, bf16[4,32,8,64]{3,1,2,0:T(8,128)(2,1)S(1)}, u32[]{:S(2)}) copy-start(bf16[4,32,8,64]{3,1,2,0:T(8,128)(2,1)S(1)} %fusion.114) | copy-start | bytes 393220
  434.9 8.7 %copy-start.30 = (bf16[4,32,2,64,1]{3,1,4,2,0:T(8,128)(2,1)}, bf16[4,32,2,64,1]{3,1,4,2,0:T(8,128)(2,1)S(1)}, u32[]{:S(2)}) copy-start(bf16[4,32,2,64,1]{3,1,4,2,0:T(8,128)(2,1)S(1)} %fusion.131) | copy-start | bytes 98308
  437.0 1.0 copy-start.15
  442.1 1.5 copy-start.33
  448.7 5.4 %copy-start.16 = (f32[4,32,2048]{2,1,0:T(8,128)S(1)}, f32[4,32,2048]{2,1,0:T(8,128)}, u32[]{:S(2)}) copy-start(f32[4,32,2048]{2,1,0:T(8,128)} %copy-done.15) | copy-start | bytes 3145732
  448.7 5.4 %copy-start.24 = (bf16[4,2,64,4,32]{2,4,3,1,0:T(8,128)(2,1)S(1)}, bf16[4,2,64,4,32]{2,4,3,1,0:T(8,128)(2,1)}, u32[]{:S(2)}) copy-start(bf16[4,2,64,4,32]{2,4,3,1,0:T(8,128)(2,1)} %convolution_convert_fusion.3) | copy-start | bytes 393220
  462.6 7.3 %copy-start.17 = (f32[1,2048,2,64]{1,3,2,0:T(8,128)S(1)}, f32[1,2048,2,64]{1,3,2,0:T(8,128)}, u32[]{:S(2)}) copy-start(f32[1,2048,2,64]{1,3,2,0:T(8,128)} %convolution_bitcast_fusion.15) | copy-start | bytes 3145732
  465.8 4.0 copy-start.18
  465.8 4.0 copy-start.19
  471.7 11.8 %copy-start = (f32[1,2048,8,64]{1,3,2,0:T(8,128)S(1)}, f32[1,2048,8,64]{1,3,2,0:T(8,128)}, u32[]{:S(2)}) copy-start(f32[1,2048,8,64]{1,3,2,0:T(8,128)} %convolution_bitcast_fusion.6) | copy-start | bytes 12582916
  511.7 4.4 copy-start.21
Sparse Core Ops, SparseCore 0:
  34.4 48.4 all-reduce.22
  115.1 45.7 all-reduce.20
  190.2 45.7 all-reduce.18
  267.1 45.7 all-reduce.16
  357.3 45.7 all-reduce.14
  465.9 45.7 all-reduce.12
where the time goes:
time: 532 us; the launch traced here: 524 us
  matrix products  231 us (43%)
  waiting for transfers between devices  152 us (29%)
  other arithmetic  122 us (23%)
  between operations  15.2 us (3%)
    psum x6, waiting for transfers between devices, tp_sum(): return lax.psum(partial_val, 'tp')  152 us
    another operation x6, other arithmetic, stack_grads(): jnp.stack([layer_grads[grad_pos] for layer_grads in grads_by_layer])  99 us
    dot_general x3, matrix products, block_back(): jnp.einsum('bsd,bsf->df', norm_g_b, d_pre, preferred_element_type=F32)  27.2 us
    dot_general x3, matrix products, block_back(): jnp.einsum('bsf,bsd->fd', act_b, dy2_b, preferred_element_type=F32)  24.4 us
    dot_general x3, matrix products, block_back(): jnp.einsum('bsf,df->bsd', d_pre, w_up, preferred_element_type=F32)  22 us
    dot_general x3, matrix products, block_back(): d_act = jnp.einsum('bsd,fd->bsf', dy2_b, w_down, preferred_element_type=F32)  19.7 us
    dot_general x3, matrix products, block_back(): jnp.einsum('bsf,fd->bsd', act_b, w_down, preferred_element_type=F32)  17.8 us
    dot_general x3, matrix products, block_back(): jnp.einsum('bsd,df->bsf', norm_g_b, w_up, preferred_element_type=F32)  14.6 us
  transfers between devices with their start and end apart: 6, of which 5 were waited for; matrix products, arithmetic and copies ran while one was open for 29% of the time, Pallas kernels for 0%

commit v1 on v0

v1 whole, which is shorter than its diff:
```python
import functools
import jax
import jax.numpy as jnp
from jax import lax
from jax.experimental import pallas as pl
from jax.experimental.pallas import tpu as pltpu
from jax.sharding import PartitionSpec as P

F32 = jnp.float32
BF16 = jnp.bfloat16
EPS = 1e-5
MASK_VALUE = -1e30
MESH = pl.DeviceIdType.MESH
GELU_C = 0.7978845608028654
GELU_A = 0.044715

G, B, FW, DW = 0, 1, 2, 3
NT = (((1,), (1,)), ((), ()))
TN = (((0,), (0,)), ((), ()))


def dot_nn(a, b):
    return jnp.dot(a, b, preferred_element_type=F32)


def dot_nt(a, b):
    return lax.dot_general(a, b, NT, preferred_element_type=F32)


def dot_tn(a, b):
    return lax.dot_general(a, b, TN, preferred_element_type=F32)


def inv_rms(x_val):
    return lax.rsqrt(jnp.mean(x_val * x_val, axis=-1, keepdims=True) + EPS)


def rms_back(x_val, grad_norm):
    r = inv_rms(x_val)
    normed = x_val * r
    return r * (grad_norm - normed * jnp.mean(grad_norm * normed, axis=-1, keepdims=True))


def chain_kernel(lens_ref, y1_ref, y2_ref, d1_ref, d2_ref, wup_ref, wdn_ref, wq_ref, wk_ref, wv_ref, wo_ref,
                 on1, oh, ou, oe, on2, oa, oc, odqkv, ofin,
                 w1, w2, wa, wo, n1b, eb, n2b, cb, hb, ub, ab, dqb, gp, qkv, pbuf,
                 part, rd, sx, rx, st,
                 s_in, s_w, s_out, s_ds, s_dr, s_xs, s_xr, s_as, s_ar, s_fin,
                 *, n_layers, seq, d_model, ff, nq, nkv, head_dim, n_chunk):
    tokens = 4 * seq
    cw = d_model // n_chunk
    fw = ff // n_chunk
    me = lax.axis_index("tp")
    xi = lax.div(me, 2)
    ci = lax.rem(me, 2)
    xo = 1 - xi
    co = 1 - ci
    x_dev = {"tp": 2 * xo + ci}
    c_dev = {"tp": 2 * xi + co}
    score_scale = head_dim ** -0.5

    def rows(slot):
        return pl.ds(pl.multiple_of(slot * seq, seq), seq)

    def w_copies(lay, group):
        if group == 0:
            return [pltpu.make_async_copy(wup_ref.at[lay], w1, s_w.at[0])]
        if group == 1:
            return [pltpu.make_async_copy(wdn_ref.at[lay], w2, s_w.at[1])]
        if group == 2:
            return [pltpu.make_async_copy(wq_ref.at[lay], wa.at[pl.ds(0, nq)], s_w.at[2]),
                    pltpu.make_async_copy(wk_ref.at[lay], wa.at[pl.ds(nq, nkv)], s_w.at[4]),
                    pltpu.make_async_copy(wv_ref.at[lay], wa.at[pl.ds(nq + nkv, nkv)], s_w.at[5])]
        return [pltpu.make_async_copy(wo_ref.at[lay], wo, s_w.at[3])]

    def w_start(lay, group):
        for cp in w_copies(lay, group):
            cp.start()

    def w_wait(lay, group):
        for cp in w_copies(lay, group):
            cp.wait()

    def cols(k):
        return pl.ds(k * cw, cw)

    def d_copy(ty, k):
        return pltpu.make_async_remote_copy(
            part.at[ty, :, co, :, cols(k)], rd.at[ty, :, :, cols(k)], s_ds.at[ty, k], s_dr.at[ty, k],
            device_id=c_dev, device_id_type=MESH)

    def x_copy(ty, k):
        return pltpu.make_async_remote_copy(
            sx.at[ty, :, cols(k)], rx.at[ty, :, cols(k)], s_xs.at[ty, k], s_xr.at[ty, k],
            device_id=x_dev, device_id_type=MESH)

    def put_part(ty, k, val):
        part[ty, :, :, :, cols(k)] = val.reshape(2, 2, seq, cw)
        d_copy(ty, k).start()

    def mid(ty, k):
        d_copy(ty, k).wait_recv()
        sx[ty, :, cols(k)] = part[ty, xo, ci, :, cols(k)] + rd[ty, xo, :, cols(k)]
        x_copy(ty, k).start()

    def fin_sum(ty):
        for k in range(n_chunk):
            x_copy(ty, k).wait_recv()
        total = part[ty, xi, ci] + rd[ty, xi] + rx[ty]
        for k in range(n_chunk):
            x_copy(ty, k).wait_send()
            d_copy(ty, k).wait_send()
        return total

    ag_buf = {G: n2b, B: cb, FW: n1b, DW: eb}

    def ag_copy(ty, lay, step):
        buf = ag_buf[ty]
        slot = 2 * xo + ci if step == 2 else me
        return pltpu.make_async_remote_copy(
            buf.at[lay, rows(slot)], buf.at[lay, rows(slot)], s_as.at[ty, step], s_ar.at[ty, step],
            device_id=x_dev if step == 0 else c_dev, device_id_type=MESH)

    def ag_start(ty, lay, val):
        ag_buf[ty][lay, rows(me)] = val
        ag_copy(ty, lay, 0).start()
        ag_copy(ty, lay, 1).start()

    def ag_forward(ty, lay):
        ag_copy(ty, lay, 0).wait_recv()
        ag_copy(ty, lay, 2).start()

    def ag_ready(ty, lay):
        ag_copy(ty, lay, 1).wait_recv()
        ag_copy(ty, lay, 2).wait_recv()
        for step in range(3):
            ag_copy(ty, lay, step).wait_send()

    outs = [(on1, n1b), (oh, hb), (ou, ub), (oe, eb), (on2, n2b), (oa, ab), (oc, cb), (odqkv, dqb)]

    def out_copy(idx, lay):
        dst, src = outs[idx]
        return pltpu.make_async_copy(src.at[lay], dst.at[lay], s_out.at[idx, lay])

    def g_up(lay):
        for k in range(n_chunk):
            pre = dot_nn(n1b[lay], w1[:, pl.ds(k * fw, fw)])
            sq = pre * pre
            th = jnp.tanh(GELU_C * (pre + GELU_A * (sq * pre)))
            cdf = 0.5 * (1.0 + th)
            hb[lay, :, pl.ds(k * fw, fw)] = (pre * cdf).astype(BF16)
            gp[:, pl.ds(k * fw, fw)] = cdf + pre * (0.5 * (1.0 - th * th)) * (GELU_C * (1.0 + (3.0 * GELU_A) * sq))

    def g_down(lay):
        for k in range(n_chunk):
            put_part(G, k, dot_nn(hb[lay], w2[:, cols(k)]))
            if k >= 1:
                mid(G, k - 1)

    def b_up(lay):
        for k in range(n_chunk):
            d_act = dot_nt(eb[lay], w2[pl.ds(k * fw, fw), :])
            ub[lay, :, pl.ds(k * fw, fw)] = (gp[:, pl.ds(k * fw, fw)] * d_act).astype(BF16)

    def b_down(lay):
        for k in range(n_chunk):
            put_part(B, k, dot_nt(ub[lay], w1[cols(k), :]))

    lane = lax.broadcasted_iota(jnp.int32, (tokens, 2 * head_dim), 1)
    left = lane < head_dim

    def halves(blk):
        blk = blk.astype(F32)
        rolled = pltpu.roll(blk, head_dim, 1)
        zero = jnp.zeros_like(blk)
        return (((jnp.where(left, blk, zero)).astype(BF16), (jnp.where(left, zero, rolled)).astype(BF16)),
                ((jnp.where(left, rolled, zero)).astype(BF16), (jnp.where(left, zero, blk)).astype(BF16)))

    def visible():
        row = lax.broadcasted_iota(jnp.int32, (tokens, tokens), 0)
        col = lax.broadcasted_iota(jnp.int32, (tokens, tokens), 1)
        row_seq = lax.div(row, seq)
        limit = jnp.zeros((tokens, tokens), jnp.int32)
        for s in range(4):
            limit = jnp.where(row_seq == s, s * seq + lens_ref[s], limit)
        return (col <= row) & (col >= row_seq * seq) & (col < limit)

    n_pairs = nq // (2 * head_dim)
    pairs_per_slot = n_pairs // 2

    def f_fwd(lay):
        qkv[...] = dot_nt(n2b[lay], wa[...]).astype(BF16)
        keys = halves(qkv[:, nq:nq + nkv])
        vals = halves(qkv[:, nq + nkv:])
        vis = visible()
        for j in range(n_pairs):
            slot = j // pairs_per_slot
            q_pair = qkv[:, j * 2 * head_dim:(j + 1) * 2 * head_dim]
            att = None
            for half in range(2):
                s_val = jnp.where(vis, dot_nt(q_pair, keys[slot][half]) * score_scale, MASK_VALUE)
                ex = jnp.exp(s_val - jnp.max(s_val, axis=-1, keepdims=True))
                prob = ex / jnp.sum(ex, axis=-1, keepdims=True)
                pbuf[2 * j + half] = prob
                term = dot_nn(prob.astype(BF16), vals[slot][half])
                att = term if att is None else att + term
            ab[lay, :, j * 2 * head_dim:(j + 1) * 2 * head_dim] = att.astype(BF16)

    def f_out(lay):
        for k in range(n_chunk):
            put_part(FW, k, dot_nn(ab[lay], wo[:, cols(k)]))
            if k >= 1:
                mid(FW, k - 1)

    def d_attn(lay):
        d_out = dot_nt(cb[lay], wo[...]).astype(BF16)
        keys = halves(qkv[:, nq:nq + nkv])
        vals = halves(qkv[:, nq + nkv:])
        acc_v = [[None, None], [None, None]]
        acc_k = [[None, None], [None, None]]
        for j in range(n_pairs):
            slot = j // pairs_per_slot
            sl = slice(j * 2 * head_dim, (j + 1) * 2 * head_dim)
            q_pair = qkv[:, sl]
            d_pair = d_out[:, sl]
            dq = None
            for half in range(2):
                prob = pbuf[2 * j + half]
                tv = dot_tn(prob.astype(BF16), d_pair)
                dp = dot_nt(d_pair, vals[slot][half])
                row_dot = jnp.sum(prob * dp, axis=-1, keepdims=True)
                ds = (prob * (dp - row_dot) * score_scale).astype(BF16)
                tk = dot_tn(ds, q_pair)
                tq = dot_nn(ds, keys[slot][half])
                dq = tq if dq is None else dq + tq
                prev = acc_v[slot][half]
                acc_v[slot][half] = tv if prev is None else prev + tv
                prev = acc_k[slot][half]
                acc_k[slot][half] = tk if prev is None else prev + tk
            dqb[lay, :, sl] = dq.astype(BF16)

        def merge(acc):
            slot0 = acc[0][0] + pltpu.roll(acc[0][1], head_dim, 1)
            slot1 = pltpu.roll(acc[1][0], head_dim, 1) + acc[1][1]
            return jnp.where(left, slot0, slot1).astype(BF16)

        dqb[lay, :, nq:nq + nkv] = merge(acc_k)
        dqb[lay, :, nq + nkv:] = merge(acc_v)

    def d_out_step(lay):
        for k in range(n_chunk):
            put_part(DW, k, dot_nn(dqb[lay], wa[:, cols(k)]))

    def g_fin(lay):
        x2 = st[1] - fin_sum(G)
        st[1] = x2
        ag_start(G, lay, (x2 * inv_rms(x2)).astype(BF16))

    def b_fin(lay):
        dy1 = st[2] + rms_back(st[0], fin_sum(B))
        st[2] = dy1
        ag_start(B, lay, dy1.astype(BF16))

    def f_fin(lay, more):
        x1 = st[0] - fin_sum(FW)
        st[0] = x1

        @pl.when(more)
        def _():
            ag_start(FW, lay - 1, (x1 * inv_rms(x1)).astype(BF16))

    def d_fin(lay, more):
        dx2 = st[3] + rms_back(st[1], fin_sum(DW))
        st[3] = dx2

        @pl.when(more)
        def _():
            ag_start(DW, lay - 1, dx2.astype(BF16))

    top = n_layers - 1
    in_full = [pltpu.make_async_copy(y1_ref, part.at[FW], s_in.at[0]),
               pltpu.make_async_copy(d2_ref, part.at[DW], s_in.at[1])]
    in_own = [pltpu.make_async_copy(src.at[xi, ci], st.at[i], s_in.at[2 + i])
              for i, src in enumerate((y1_ref, y2_ref, d1_ref, d2_ref))]
    in_full[0].start()
    w_start(top, 0)
    in_full[1].start()
    w_start(top, 1)
    for cp in in_own:
        cp.start()
    w_start(top, 2)
    w_start(top, 3)
    barrier = pltpu.get_barrier_semaphore()
    pl.semaphore_signal(barrier, inc=1, device_id=x_dev, device_id_type=MESH)
    pl.semaphore_signal(barrier, inc=1, device_id=c_dev, device_id_type=MESH)
    in_full[0].wait()
    for a in range(2):
        for b in range(2):
            y_val = part[FW, a, b]
            n1b[top, pl.ds((2 * a + b) * seq, seq)] = (y_val * inv_rms(y_val)).astype(BF16)
    in_full[1].wait()
    for a in range(2):
        for b in range(2):
            eb[top, pl.ds((2 * a + b) * seq, seq)] = part[DW, a, b].astype(BF16)
    for cp in in_own:
        cp.wait()
    pl.semaphore_wait(barrier, 2)

    def layer_body(i, carry):
        lay = top - i
        more = i < top
        not_first = i > 0
        w_wait(lay, 0)
        g_up(lay)
        out_copy(0, lay).start()
        out_copy(1, lay).start()
        w_wait(lay, 1)
        g_down(lay)

        @pl.when(not_first)
        def _():
            d_fin(lay + 1, True)

        mid(G, n_chunk - 1)

        @pl.when(not_first)
        def _():
            ag_forward(DW, lay)
            ag_ready(DW, lay)

        b_up(lay)
        b_down(lay)
        out_copy(2, lay).start()
        out_copy(3, lay).start()

        @pl.when(more)
        def _():
            w_start(lay - 1, 0)
            w_start(lay - 1, 1)

        g_fin(lay)
        for k in range(n_chunk):
            mid(B, k)
        ag_forward(G, lay)
        ag_ready(G, lay)
        out_copy(4, lay).start()
        w_wait(lay, 2)
        f_fwd(lay)
        w_wait(lay, 3)
        f_out(lay)
        out_copy(5, lay).start()
        mid(FW, n_chunk - 1)
        b_fin(lay)
        ag_forward(B, lay)
        ag_ready(B, lay)
        out_copy(6, lay).start()
        d_attn(lay)
        d_out_step(lay)
        out_copy(7, lay).start()

        @pl.when(more)
        def _():
            w_start(lay - 1, 2)
            w_start(lay - 1, 3)

        f_fin(lay, more)
        for k in range(n_chunk):
            mid(DW, k)

        @pl.when(more)
        def _():
            ag_forward(FW, lay - 1)
            ag_ready(FW, lay - 1)

        return carry

    lax.fori_loop(0, n_layers, layer_body, 0)
    d_fin(0, False)
    fin = pltpu.make_async_copy(st, ofin, s_fin)
    fin.start()
    for idx in range(8):
        for lay in range(n_layers):
            out_copy(idx, lay).wait()
    fin.wait()


def run_chain(lens, y1, y2, d1, d2, w_up, w_down, wq, wk, wv, wo):
    n_layers, d_model, ff = w_up.shape
    seq = y1.shape[2]
    tokens = 4 * seq
    nq, nkv = wq.shape[1], wk.shape[1]
    head_dim = nkv // 2
    n_chunk = 4
    n_w = nq + 2 * nkv
    body = functools.partial(chain_kernel, n_layers=n_layers, seq=seq, d_model=d_model, ff=ff, nq=nq, nkv=nkv,
                             head_dim=head_dim, n_chunk=n_chunk)
    any_spec = pl.BlockSpec(memory_space=pl.ANY)
    wide = jax.ShapeDtypeStruct((n_layers, tokens, d_model), BF16)
    wide_ff = jax.ShapeDtypeStruct((n_layers, tokens, ff), BF16)
    out_shape = [wide, wide_ff, wide_ff, wide, wide, jax.ShapeDtypeStruct((n_layers, tokens, nq), BF16), wide,
                 jax.ShapeDtypeStruct((n_layers, tokens, n_w), BF16),
                 jax.ShapeDtypeStruct((4, seq, d_model), F32)]
    vm = pltpu.VMEM
    dma = pltpu.SemaphoreType.DMA
    scratch = [vm((d_model, ff), BF16), vm((ff, d_model), BF16), vm((n_w, d_model), BF16), vm((nq, d_model), BF16),
               vm((n_layers, tokens, d_model), BF16), vm((n_layers, tokens, d_model), BF16),
               vm((n_layers, tokens, d_model), BF16), vm((n_layers, tokens, d_model), BF16),
               vm((n_layers, tokens, ff), BF16), vm((n_layers, tokens, ff), BF16),
               vm((n_layers, tokens, nq), BF16), vm((n_layers, tokens, n_w), BF16),
               vm((tokens, ff), F32), vm((tokens, n_w), BF16), vm((nq // head_dim, tokens, tokens), F32),
               vm((4, 2, 2, seq, d_model), F32), vm((4, 2, seq, d_model), F32),
               vm((4, seq, d_model), F32), vm((4, seq, d_model), F32), vm((4, seq, d_model), F32),
               dma((6,)), dma((6,)), dma((8, n_layers)),
               dma((4, n_chunk)), dma((4, n_chunk)), dma((4, n_chunk)), dma((4, n_chunk)),
               dma((4, 3)), dma((4, 3)), dma]
    return pl.pallas_call(
        body, out_shape=out_shape,
        in_specs=[pl.BlockSpec(memory_space=pltpu.SMEM)] + [any_spec] * 10,
        out_specs=[any_spec] * 9,
        scratch_shapes=scratch,
        compiler_params=pltpu.CompilerParams(collective_id=0, has_side_effects=True, vmem_limit_bytes=60 * 2 ** 20),
        cost_estimate=pl.CostEstimate(flops=60 * 10 ** 9, bytes_accessed=10 ** 8, transcendentals=0),
        name="chain",
    )(lens, y1, y2, d1, d2, w_up, w_down, wq, wk, wv, wo)


def ff_grad_kernel(n1_ref, u_ref, h_ref, e_ref, dup_ref, ddn_ref):
    dup_ref[0] = dot_tn(n1_ref[0], u_ref[0])
    ddn_ref[0] = dot_tn(h_ref[0], e_ref[0])


def ff_grads(n1, u, h, e):
    n_layers, tokens, d_model = n1.shape
    ff = u.shape[2]
    n_tiles = 8
    rd, rf = d_model // n_tiles, ff // n_tiles
    return pl.pallas_call(
        ff_grad_kernel, grid=(n_layers, n_tiles),
        out_shape=[jax.ShapeDtypeStruct((n_layers, d_model, ff), F32), jax.ShapeDtypeStruct((n_layers, ff, d_model), F32)],
        in_specs=[pl.BlockSpec((1, tokens, rd), lambda l, t: (l, 0, t)), pl.BlockSpec((1, tokens, ff), lambda l, t: (l, 0, 0)),
                  pl.BlockSpec((1, tokens, rf), lambda l, t: (l, 0, t)), pl.BlockSpec((1, tokens, d_model), lambda l, t: (l, 0, 0))],
        out_specs=[pl.BlockSpec((1, rd, ff), lambda l, t: (l, t, 0)), pl.BlockSpec((1, rf, d_model), lambda l, t: (l, t, 0))],
        compiler_params=pltpu.CompilerParams(dimension_semantics=("arbitrary", "arbitrary")),
        cost_estimate=pl.CostEstimate(flops=30 * 10 ** 9, bytes_accessed=10 ** 8, transcendentals=0),
        name="ff_grads",
    )(n1, u, h, e)


def attn_grad_kernel(dqkv_ref, n2_ref, a_ref, c_ref, dq_ref, dk_ref, dv_ref, do_ref, *, nq, nkv):
    n2 = n2_ref[0]
    dq_ref[0] = dot_tn(dqkv_ref[0, :, :nq], n2)
    dk_ref[0] = dot_tn(dqkv_ref[0, :, nq:nq + nkv], n2)
    dv_ref[0] = dot_tn(dqkv_ref[0, :, nq + nkv:], n2)
    do_ref[0] = dot_tn(a_ref[0], c_ref[0])


def attn_grads(dqkv, n2, a, c, nq, nkv):
    n_layers, tokens, d_model = n2.shape
    n_tiles = 2
    cw = d_model // n_tiles
    n_w = nq + 2 * nkv
    return pl.pallas_call(
        functools.partial(attn_grad_kernel, nq=nq, nkv=nkv), grid=(n_layers, n_tiles),
        out_shape=[jax.ShapeDtypeStruct((n_layers, r, d_model), F32) for r in (nq, nkv, nkv, nq)],
        in_specs=[pl.BlockSpec((1, tokens, n_w), lambda l, t: (l, 0, 0)), pl.BlockSpec((1, tokens, cw), lambda l, t: (l, 0, t)),
                  pl.BlockSpec((1, tokens, nq), lambda l, t: (l, 0, 0)), pl.BlockSpec((1, tokens, cw), lambda l, t: (l, 0, t))],
        out_specs=[pl.BlockSpec((1, r, cw), lambda l, t: (l, 0, t)) for r in (nq, nkv, nkv, nq)],
        compiler_params=pltpu.CompilerParams(dimension_semantics=("arbitrary", "arbitrary")),
        cost_estimate=pl.CostEstimate(flops=10 * 10 ** 9, bytes_accessed=3 * 10 ** 7, transcendentals=0),
        name="attn_grads",
    )(dqkv, n2, a, c)


def gather_tp(own):
    me = lax.axis_index("tp")
    across = lax.ppermute(own, "tp", [(0, 2), (2, 0), (1, 3), (3, 1)])
    chip = jnp.stack([own, across])
    other = lax.ppermute(chip, "tp", [(0, 1), (1, 0), (2, 3), (3, 2)])
    own_chip = jnp.where(me < 2, chip, chip[::-1])
    oth_chip = jnp.where(me < 2, other, other[::-1])
    even = lax.rem(me, 2) == 0
    first = jnp.where(even, own_chip, oth_chip)
    second = jnp.where(even, oth_chip, own_chip)
    return [jnp.stack([first[0, i], second[0, i], first[1, i], second[1, i]]) for i in range(4)]


def solution(mesh):
    act_spec = P('dp', None, None)
    w_specs = (P(None, None, 'tp', None), P(None, None, 'tp', None), P(None, None, 'tp', None),
               P(None, 'tp', None, None), P(None, None, 'tp'), P(None, 'tp', None))
    g_specs = (P('dp', None, 'tp', None), P('dp', None, 'tp', None), P('dp', None, 'tp', None),
               P('dp', 'tp', None, None), P('dp', None, 'tp'), P('dp', 'tp', None))

    def local_fn(y_one, y_two, dy_one, dy_two, seq_lens, w_query, w_key, w_value, w_out, w_up, w_down):
        n_layers, d_model, heads, head_dim = w_query.shape
        slots = w_key.shape[2]
        seq = y_one.shape[1]
        nq, nkv = heads * head_dim, slots * head_dim

        def to_rows(w, width):
            return jnp.transpose(w, (0, 2, 3, 1)).reshape(n_layers, width, d_model)

        def from_rows(g, n_heads):
            return jnp.transpose(g.reshape(n_layers, n_heads, head_dim, d_model), (0, 3, 1, 2))

        acts = [a.reshape(2, 2, seq, d_model) for a in (y_one, y_two, dy_one, dy_two)]
        n1, h, u, e, n2, a, c, dqkv, fin = run_chain(
            seq_lens, *acts, w_up, w_down, to_rows(w_query, nq), to_rows(w_key, nkv), to_rows(w_value, nkv),
            w_out.reshape(n_layers, nq, d_model))
        gathered = gather_tp(fin)
        d_up, d_down = ff_grads(n1, u, h, e)
        dq, dk, dv, do = attn_grads(dqkv, n2, a, c, nq, nkv)
        outs = gathered
        return (outs[0], outs[1], outs[2], outs[3],
                from_rows(dq, heads), from_rows(dk, slots), from_rows(dv, slots),
                do.reshape(n_layers, heads, head_dim, d_model), d_up, d_down)

    return jax.shard_map(local_fn, mesh=mesh,
                         in_specs=(act_spec,) * 4 + (P('dp'),) + w_specs,
                         out_specs=(act_spec,) * 4 + g_specs,
                         check_vma=False)
```

time: 532 us -> 231 us (0.43); the launches traced: 524 us -> 230 us
  matrix products: 231 us -> 0 us
  Pallas kernels: 0 us -> 208 us
  waiting for transfers between devices: 152 us -> 11.2 us
  other arithmetic: 122 us -> 8.4 us
  between operations: 15.2 us -> 0.69 us
    dot_general x69 -> x0, matrix products: 227 us -> none  [the longest x3 27.2 us: block_back(): jnp.einsum('bsd,bsf->df', norm_g_b, d_pre, preferred_element_type=F32)]
    pallas_call x0 -> x3, Pallas kernels: none -> 208 us  [the longest x1 161 us: run_chain(): pl.pallas_call(body, out_shape=out_shape, in_specs=[pl.BlockSpec(memory_s...]
    psum x6 -> x0, waiting for transfers between devices: 152 us -> none  [tp_sum(): return lax.psum(partial_val, 'tp')]
    another operation x6 -> x5, other arithmetic: 99 us -> 5.57 us  [the longest x4 4.17 us: gather_tp(): jnp.stack([first[0, i], second[0, i], first[1, i], second[1, i]])]
    reduce_sum x12 -> x0, other arithmetic: 14.2 us -> none  [the longest x6 7.48 us: rms_norm(): inv_rms = lax.rsqrt(jnp.mean(x_val * x_val, axis=-1, keepdims=True) + EPS)]
    ppermute x0 -> x2, waiting for transfers between devices: none -> 11.2 us  [the longest x1 11.2 us: gather_tp(): across = lax.ppermute(own, 'tp', [(0, 2), (2, 0), (1, 3), (3, 1)])]
    add x5 -> x0, other arithmetic: 6.67 us -> none  [the longest x3 6.08 us: block_back(): dx_two = dy_two + rms_back(norm_f, inv_f, grad_norm_f)]
  transfers between devices with their start and end apart: 6 -> 2, of which waited for: 5 -> 1; matrix products, arithmetic and copies ran while one was open for 29% -> 0% of each run, Pallas kernels for 0% -> 21%
where the time goes in v1:
time: 231 us; the launch traced here: 230 us
  Pallas kernels  208 us (90%)
  waiting for transfers between devices  11.2 us (5%)
  other arithmetic  8.4 us (4%)
    pallas_call x1, Pallas kernels, run_chain(): pl.pallas_call(body, out_shape=out_shape, in_specs=[pl.BlockSpec(memory_s...  161 us
    pallas_call x1, Pallas kernels, ff_grads(): pl.pallas_call(ff_grad_kernel, grid=(n_layers, n_tiles), out_shape=[jax.S...  34.5 us
    pallas_call x1, Pallas kernels, attn_grads(): pl.pallas_call(functools.partial(attn_grad_kernel, nq=nq, nkv=nkv), grid=...  12.8 us
    ppermute x1, waiting for transfers between devices, gather_tp(): across = lax.ppermute(own, 'tp', [(0, 2), (2, 0), (1, 3), (3, 1)])  11.2 us
  transfers between devices with their start and end apart: 2, of which 1 were waited for; matrix products, arithmetic and copies ran while one was open for 0% of the time, Pallas kernels for 21%

profile of v1, /device:TPU:0, one launch (start us, length us, event | category | flops | bytes accessed | tf_op | source)
XLA Modules:
  0.0 230.4 jit_solution(3291864833865030806)
XLA Ops:
  0.6 160.6 %chain.1 = (bf16[3,128,2048]{2,1,0:T(8,128)(2,1)}, bf16[3,128,2048]{2,1,0:T(8,128)(2,1)}, bf16[3,128,2048]{2,1,0:T(8,128)(2,1)}, bf16[3,128,2048]{2,1,0:T(8,128)...) custom-call(s32[4]{0:T(128)} %lens_ref.1, ...), custom_call_target="tpu_custom_call" | custom-call | flops 60000002048 | bytes 100000000 | tf_op jit(solution)/shard_map/chain/pallas_call | solution.py:416
  161.2 0.6 collective-permute-start
  161.9 0.0 copy-start
  161.9 12.8 %attn_grads.1 = (f32[3,512,2048]{2,1,0:T(8,128)}, f32[3,128,2048]{2,1,0:T(8,128)}, f32[3,128,2048]{2,1,0:T(8,128)}, f32[3,512,2048]{2,1,0:T(8,128)}) custom-call(bf16[3,128,768]{2,1,0:T(8,128)(2,1)} %get-tuple-element.26.dqkv_ref, bf16[3,128,2048]{2,1,0:T(8,128)(2,1)} %get-tuple-element.27.n2_ref, bf16[3,128,512]{2,1,0:T(8,128)(2,1)} %get-tuple-element.28.a_ref, ...), custom_call_target="tpu_custom_call" | custom-call | flops 10000000000 | bytes 30000000 | tf_op jit(solution)/shard_map/attn_grads/pallas_call | solution.py:462
  174.7 11.2 %collective-permute-done = f32[4,32,2048]{2,1,0:T(8,128)S(1)} collective-permute-done((f32[4,32,2048]{2,1,0:T(8,128)}, f32[4,32,2048]{2,1,0:T(8,128)S(1)}, u32[]{:S(2)}, u32[]{:S(2)}) %collective-permute-start) | collective-permute-done | bytes 1048608 | tf_op jit(solution)/shard_map/ppermute | solution.py:476
  185.9 0.0 copy-start.1
  185.9 1.0 copy-done.1
  186.9 0.0 copy-done
  186.9 1.4 pad_maximum_fusion
  188.3 0.0 collective-permute-start.1
  188.3 34.5 %ff_grads.1 = (f32[3,2048,2048]{2,1,0:T(8,128)}, f32[3,2048,2048]{2,1,0:T(8,128)}) custom-call(bf16[3,128,2048]{2,1,0:T(8,128)(2,1)} %get-tuple-element.34.n1_ref, bf16[3,128,2048]{2,1,0:T(8,128)(2,1)} %get-tuple-element.35.u_ref, bf16[3,128,2048]{2,1,0:T(8,128)(2,1)} %get-tuple-element.36.h_ref, bf16[3,128,2048]{2,1,0:T(8,128)(2,1)} %get-tuple-element.37.e_ref), custom_call_target="tpu_custom_call" | custom-call | flops 30000001024 | bytes 100000000 | tf_op jit(solution)/shard_map/ff_grads/pallas_call | solution.py:437
  222.8 0.0 collective-permute-done.1
  222.8 2.8 %fusion.1 = (f32[2,4,32,2048]{3,2,1,0:T(8,128)S(1)}, f32[2,4,32,2048]{3,2,1,0:T(8,128)S(1)}) fusion(f32[2,4,32,2048]{3,2,1,0:T(8,128)S(1)} %pad_maximum_fusion, f32[2,4,32,2048]{3,2,1,0:T(8,128)} %collective-permute-done.1, pred[]{:T(512)S(6)} %lt.4, pred[]{:T(512)S(6)} %eq.3), kind=kLoop, calls=%fused_computation.4 | loop fusion | flops 2097152 | bytes 8388610 | tf_op jit(solution)/shard_map/jit(_where)/select_n | solution.py:482
  225.7 0.5 slice_bitcast_fusion.2
  226.2 1.0 pad_maximum_fusion.4
  227.2 1.0 pad_maximum_fusion.3
  228.3 1.0 pad_maximum_fusion.2
  229.3 1.0 pad_maximum_fusion.1
Async XLA Ops:
  161.2 24.7 %collective-permute-start = (f32[4,32,2048]{2,1,0:T(8,128)}, f32[4,32,2048]{2,1,0:T(8,128)S(1)}, u32[]{:S(2)}, u32[]{:S(2)}) collective-permute-start(f32[4,32,2048]{2,1,0:T(8,128)} %get-tuple-element.25), channel_id=1, source_target_pairs={{0,2},{2,0},{1,3},{3,1},{4,6},{6,4},{5,7},{7,5}} | collective-permute-start | bytes 3145736 | tf_op jit(solution)/shard_map/ppermute | solution.py:476
  161.9 25.0 %copy-start = (f32[4,32,2048]{2,1,0:T(8,128)S(1)}, f32[4,32,2048]{2,1,0:T(8,128)}, u32[]{:S(2)}) copy-start(f32[4,32,2048]{2,1,0:T(8,128)} %get-tuple-element.25) | copy-start | bytes 3145732
  185.9 1.0 copy-start.1
  188.3 34.6 %collective-permute-start.1 = (f32[2,4,32,2048]{3,2,1,0:T(8,128)S(1)}, f32[2,4,32,2048]{3,2,1,0:T(8,128)}, u32[]{:S(2)}, u32[]{:S(2)}) collective-permute-start(f32[2,4,32,2048]{3,2,1,0:T(8,128)S(1)} %pad_maximum_fusion), channel_id=1, source_target_pairs={{0,1},{1,0},{2,3},{3,2},{4,5},{5,4},{6,7},{7,6}} | collective-permute-start | bytes 6291464 | tf_op jit(solution)/shard_map/ppermute | solution.py:478

commit v2 on v1

--- a/solution.py
+++ b/solution.py
@@ -62,16 +62,24 @@
     def rows(slot):
         return pl.ds(pl.multiple_of(slot * seq, seq), seq)
 
+    W_ATT = 2 * n_chunk
+    W_OUT = W_ATT + 1
+
+    def cols(k):
+        return pl.ds(k * cw, cw)
+
     def w_copies(lay, group):
-        if group == 0:
-            return [pltpu.make_async_copy(wup_ref.at[lay], w1, s_w.at[0])]
-        if group == 1:
-            return [pltpu.make_async_copy(wdn_ref.at[lay], w2, s_w.at[1])]
-        if group == 2:
-            return [pltpu.make_async_copy(wq_ref.at[lay], wa.at[pl.ds(0, nq)], s_w.at[2]),
-                    pltpu.make_async_copy(wk_ref.at[lay], wa.at[pl.ds(nq, nkv)], s_w.at[4]),
-                    pltpu.make_async_copy(wv_ref.at[lay], wa.at[pl.ds(nq + nkv, nkv)], s_w.at[5])]
-        return [pltpu.make_async_copy(wo_ref.at[lay], wo, s_w.at[3])]
+        if group < n_chunk:
+            sl = pl.ds(group * fw, fw)
+            return [pltpu.make_async_copy(wup_ref.at[lay, :, sl], w1.at[:, sl], s_w.at[group])]
+        if group < 2 * n_chunk:
+            return [pltpu.make_async_copy(wdn_ref.at[lay, :, cols(group - n_chunk)], w2.at[:, cols(group - n_chunk)],
+                                          s_w.at[group])]
+        if group == W_ATT:
+            return [pltpu.make_async_copy(wq_ref.at[lay], wa.at[pl.ds(0, nq)], s_w.at[group]),
+                    pltpu.make_async_copy(wk_ref.at[lay], wa.at[pl.ds(nq, nkv)], s_w.at[group + 2]),
+                    pltpu.make_async_copy(wv_ref.at[lay], wa.at[pl.ds(nq + nkv, nkv)], s_w.at[group + 3])]
+        return [pltpu.make_async_copy(wo_ref.at[lay], wo, s_w.at[group])]
 
     def w_start(lay, group):
         for cp in w_copies(lay, group):
@@ -80,9 +88,6 @@
     def w_wait(lay, group):
         for cp in w_copies(lay, group):
             cp.wait()
-
-    def cols(k):
-        return pl.ds(k * cw, cw)
 
     def d_copy(ty, k):
         return pltpu.make_async_remote_copy(
@@ -144,6 +149,7 @@
 
     def g_up(lay):
         for k in range(n_chunk):
+            w_wait(lay, k)
             pre = dot_nn(n1b[lay], w1[:, pl.ds(k * fw, fw)])
             sq = pre * pre
             th = jnp.tanh(GELU_C * (pre + GELU_A * (sq * pre)))
@@ -151,20 +157,16 @@
             hb[lay, :, pl.ds(k * fw, fw)] = (pre * cdf).astype(BF16)
             gp[:, pl.ds(k * fw, fw)] = cdf + pre * (0.5 * (1.0 - th * th)) * (GELU_C * (1.0 + (3.0 * GELU_A) * sq))
 
-    def g_down(lay):
-        for k in range(n_chunk):
-            put_part(G, k, dot_nn(hb[lay], w2[:, cols(k)]))
-            if k >= 1:
-                mid(G, k - 1)
-
-    def b_up(lay):
-        for k in range(n_chunk):
-            d_act = dot_nt(eb[lay], w2[pl.ds(k * fw, fw), :])
-            ub[lay, :, pl.ds(k * fw, fw)] = (gp[:, pl.ds(k * fw, fw)] * d_act).astype(BF16)
-
-    def b_down(lay):
-        for k in range(n_chunk):
-            put_part(B, k, dot_nt(ub[lay], w1[cols(k), :]))
+    def g_put(lay, k):
+        w_wait(lay, n_chunk + k)
+        put_part(G, k, dot_nn(hb[lay], w2[:, cols(k)]))
+
+    def b_up(lay, k):
+        d_act = dot_nt(eb[lay], w2[pl.ds(k * fw, fw), :])
+        ub[lay, :, pl.ds(k * fw, fw)] = (gp[:, pl.ds(k * fw, fw)] * d_act).astype(BF16)
+
+    def b_put(lay, k):
+        put_part(B, k, dot_nt(ub[lay], w1[cols(k), :]))
 
     lane = lax.broadcasted_iota(jnp.int32, (tokens, 2 * head_dim), 1)
     left = lane < head_dim
@@ -188,8 +190,10 @@
     n_pairs = nq // (2 * head_dim)
     pairs_per_slot = n_pairs // 2
 
-    def f_fwd(lay):
+    def f_proj(lay):
         qkv[...] = dot_nt(n2b[lay], wa[...]).astype(BF16)
+
+    def f_attn(lay):
         keys = halves(qkv[:, nq:nq + nkv])
         vals = halves(qkv[:, nq + nkv:])
         vis = visible()
@@ -206,11 +210,8 @@
                 att = term if att is None else att + term
             ab[lay, :, j * 2 * head_dim:(j + 1) * 2 * head_dim] = att.astype(BF16)
 
-    def f_out(lay):
-        for k in range(n_chunk):
-            put_part(FW, k, dot_nn(ab[lay], wo[:, cols(k)]))
-            if k >= 1:
-                mid(FW, k - 1)
+    def f_put(lay, k):
+        put_part(FW, k, dot_nn(ab[lay], wo[:, cols(k)]))
 
     def d_attn(lay):
         d_out = dot_nt(cb[lay], wo[...]).astype(BF16)
@@ -247,9 +248,8 @@
         dqb[lay, :, nq:nq + nkv] = merge(acc_k)
         dqb[lay, :, nq + nkv:] = merge(acc_v)
 
-    def d_out_step(lay):
-        for k in range(n_chunk):
-            put_part(DW, k, dot_nn(dqb[lay], wa[:, cols(k)]))
+    def d_put(lay, k):
+        put_part(DW, k, dot_nn(dqb[lay], wa[:, cols(k)]))
 
     def g_fin(lay):
         x2 = st[1] - fin_sum(G)
@@ -264,17 +264,13 @@
     def f_fin(lay, more):
         x1 = st[0] - fin_sum(FW)
         st[0] = x1
-
-        @pl.when(more)
-        def _():
+        if more:
             ag_start(FW, lay - 1, (x1 * inv_rms(x1)).astype(BF16))
 
     def d_fin(lay, more):
         dx2 = st[3] + rms_back(st[1], fin_sum(DW))
         st[3] = dx2
-
-        @pl.when(more)
-        def _():
+        if more:
             ag_start(DW, lay - 1, dx2.astype(BF16))
 
     top = n_layers - 1
@@ -283,13 +279,13 @@
     in_own = [pltpu.make_async_copy(src.at[xi, ci], st.at[i], s_in.at[2 + i])
               for i, src in enumerate((y1_ref, y2_ref, d1_ref, d2_ref))]
     in_full[0].start()
-    w_start(top, 0)
+    for k in range(2 * n_chunk):
+        w_start(top, k)
     in_full[1].start()
-    w_start(top, 1)
     for cp in in_own:
         cp.start()
-    w_start(top, 2)
-    w_start(top, 3)
+    w_start(top, W_ATT)
+    w_start(top, W_OUT)
     barrier = pltpu.get_barrier_semaphore()
     pl.semaphore_signal(barrier, inc=1, device_id=x_dev, device_id_type=MESH)
     pl.semaphore_signal(barrier, inc=1, device_id=c_dev, device_id_type=MESH)
@@ -298,83 +294,107 @@
         for b in range(2):
             y_val = part[FW, a, b]
             n1b[top, pl.ds((2 * a + b) * seq, seq)] = (y_val * inv_rms(y_val)).astype(BF16)
-    in_full[1].wait()
-    for a in range(2):
-        for b in range(2):
-            eb[top, pl.ds((2 * a + b) * seq, seq)] = part[DW, a, b].astype(BF16)
-    for cp in in_own:
-        cp.wait()
     pl.semaphore_wait(barrier, 2)
 
     def layer_body(i, carry):
         lay = top - i
         more = i < top
-        not_first = i > 0
-        w_wait(lay, 0)
+        first = i == 0
+        later = i > 0
+
+        @pl.when(later)
+        def _():
+            f_fin(lay + 1, True)
+            d_fin(lay + 1, True)
+            ag_forward(FW, lay)
+            ag_ready(FW, lay)
+
         g_up(lay)
         out_copy(0, lay).start()
         out_copy(1, lay).start()
-        w_wait(lay, 1)
-        g_down(lay)
-
-        @pl.when(not_first)
-        def _():
-            d_fin(lay + 1, True)
-
-        mid(G, n_chunk - 1)
-
-        @pl.when(not_first)
+        g_put(lay, 0)
+
+        @pl.when(later)
         def _():
             ag_forward(DW, lay)
+
+        g_put(lay, 1)
+        g_put(lay, 2)
+        mid(G, 0)
+        g_put(lay, 3)
+        mid(G, 1)
+
+        @pl.when(later)
+        def _():
             ag_ready(DW, lay)
 
-        b_up(lay)
-        b_down(lay)
+        @pl.when(first)
+        def _():
+            in_full[1].wait()
+            for a in range(2):
+                for b in range(2):
+                    eb[top, pl.ds((2 * a + b) * seq, seq)] = part[DW, a, b].astype(BF16)
+            for cp in in_own:
+                cp.wait()
+
+        b_up(lay, 0)
+        mid(G, 2)
+        mid(G, 3)
+        for k in range(1, n_chunk):
+            b_up(lay, k)
         out_copy(2, lay).start()
         out_copy(3, lay).start()
+        b_put(lay, 0)
+        b_put(lay, 1)
+        mid(B, 0)
+        b_put(lay, 2)
+        b_put(lay, 3)
 
         @pl.when(more)
         def _():
-            w_start(lay - 1, 0)
-            w_start(lay - 1, 1)
-
+            for k in range(2 * n_chunk):
+                w_start(lay - 1, k)
+
+        mid(B, 1)
+        mid(B, 2)
         g_fin(lay)
-        for k in range(n_chunk):
-            mid(B, k)
+        mid(B, 3)
         ag_forward(G, lay)
+        b_fin(lay)
         ag_ready(G, lay)
         out_copy(4, lay).start()
-        w_wait(lay, 2)
-        f_fwd(lay)
-        w_wait(lay, 3)
-        f_out(lay)
+        w_wait(lay, W_ATT)
+        f_proj(lay)
+        f_attn(lay)
         out_copy(5, lay).start()
-        mid(FW, n_chunk - 1)
-        b_fin(lay)
+        w_wait(lay, W_OUT)
+        f_put(lay, 0)
+        f_put(lay, 1)
+        f_put(lay, 2)
+        f_put(lay, 3)
+        mid(FW, 0)
+        mid(FW, 1)
         ag_forward(B, lay)
+        mid(FW, 2)
+        mid(FW, 3)
         ag_ready(B, lay)
         out_copy(6, lay).start()
         d_attn(lay)
-        d_out_step(lay)
         out_copy(7, lay).start()
+        for k in range(n_chunk):
+            d_put(lay, k)
 
         @pl.when(more)
         def _():
-            w_start(lay - 1, 2)
-            w_start(lay - 1, 3)
-
-        f_fin(lay, more)
+            w_start(lay - 1, W_ATT)
+            w_start(lay - 1, W_OUT)
+
         for k in range(n_chunk):
             mid(DW, k)
-
-        @pl.when(more)
-        def _():
-            ag_forward(FW, lay - 1)
-            ag_ready(FW, lay - 1)
-
         return carry
 
     lax.fori_loop(0, n_layers, layer_body, 0)
+    f_fin(0, False)
     d_fin(0, False)
     fin = pltpu.make_async_copy(st, ofin, s_fin)
     fin.start()
@@ -410,7 +430,7 @@
                vm((tokens, ff), F32), vm((tokens, n_w), BF16), vm((nq // head_dim, tokens, tokens), F32),
                vm((4, 2, 2, seq, d_model), F32), vm((4, 2, seq, d_model), F32),
                vm((4, seq, d_model), F32), vm((4, seq, d_model), F32), vm((4, seq, d_model), F32),
-               dma((6,)), dma((6,)), dma((8, n_layers)),
+               dma((6,)), dma((2 * n_chunk + 4,)), dma((8, n_layers)),
                dma((4, n_chunk)), dma((4, n_chunk)), dma((4, n_chunk)), dma((4, n_chunk)),
                dma((4, 3)), dma((4, 3)), dma]
     return pl.pallas_call(
@@ -424,64 +444,128 @@
     )(lens, y1, y2, d1, d2, w_up, w_down, wq, wk, wv, wo)
 
 
-def ff_grad_kernel(n1_ref, u_ref, h_ref, e_ref, dup_ref, ddn_ref):
+def grad_kernel(*refs, nq, nkv, n_tiles, start, n_prev, has_acts):
+    n1_ref, u_ref, h_ref, e_ref, dqkv_ref, n2_ref, a_ref, c_ref = refs[:8]
+    pos = 8
+    if has_acts:
+        srcs = refs[pos:pos + 4]
+        pos += 4
+    pos += n_prev
+    dup_ref, ddn_ref, dq_ref, dk_ref, dv_ref, do_ref = refs[pos:pos + 6]
+    pos += 6
+    idx = pl.program_id(0)
+    step = lax.rem(idx + start, n_tiles)
     dup_ref[0] = dot_tn(n1_ref[0], u_ref[0])
     ddn_ref[0] = dot_tn(h_ref[0], e_ref[0])
-
-
-def ff_grads(n1, u, h, e):
+    tile = pl.ds(pl.multiple_of(lax.div(step, 2) * 128, 128), 128)
+
+    @pl.when(lax.rem(step, 2) == 0)
+    def _():
+        dq_ref[0] = dot_tn(dqkv_ref[0, :, tile], n2_ref[0])
+
+    @pl.when(lax.rem(step, 2) == 1)
+    def _():
+        do_ref[0] = dot_tn(a_ref[0, :, tile], c_ref[0])
+
+    @pl.when((step == 1) | (idx == 0))
+    def _():
+        dk_ref[0] = dot_tn(dqkv_ref[0, :, nq:nq + nkv], n2_ref[0])
+
+    @pl.when((step == 2) | (idx == 0))
+    def _():
+        dv_ref[0] = dot_tn(dqkv_ref[0, :, nq + nkv:], n2_ref[0])
+
+    if has_acts:
+        out_refs = refs[pos:pos + 4]
+        buf, s_ld, s_st = refs[pos + 4:]
+        me = lax.axis_index("tp")
+        xi, ci = lax.div(me, 2), lax.rem(me, 2)
+        slots = (me, 2 * (1 - xi) + ci, 2 * xi + 1 - ci, 2 * (1 - xi) + 1 - ci)
+
+        def load(i):
+            return pltpu.make_async_copy(srcs[i], buf.at[i], s_ld.at[i])
+
+        def store(i, j):
+            return pltpu.make_async_copy(buf.at[i, j], out_refs[j].at[slots[i]], s_st.at[i, j])
+
+        @pl.when(idx == 0)
+        def _():
+            for i in range(4):
+                load(i).start()
+
+        @pl.when(idx == 2)
+        def _():
+            for i in range(4):
+                load(i).wait()
+                for j in range(4):
+                    store(i, j).start()
+
+        @pl.when(idx == 5)
+        def _():
+            for i in range(4):
+                for j in range(4):
+                    store(i, j).wait()
+
+
+def weight_grads(ops, start, count, nq, nkv, prev=None, acts=None):
+    n1, u, h, e, dqkv, n2, a, c = ops
     n_layers, tokens, d_model = n1.shape
     ff = u.shape[2]
-    n_tiles = 8
+    n_tiles = 2 * nq // 128
     rd, rf = d_model // n_tiles, ff // n_tiles
+    n_w = nq + 2 * nkv
+
+    def lay(i):
+        return (i + start) // n_tiles
+
+    def tile_of(i):
+        return (i + start) % n_tiles
+
+    def full(width):
+        return pl.BlockSpec((1, tokens, width), lambda i: (lay(i), 0, 0))
+
+    def tile(width):
+        return pl.BlockSpec((1, tokens, width), lambda i: (lay(i), 0, tile_of(i)))
+
+    def rows(n_rows, width):
+        return pl.BlockSpec((1, n_rows, width), lambda i: (lay(i), tile_of(i), 0))
+
+    def half(n_rows, width):
+        return pl.BlockSpec((1, n_rows, width), lambda i: (lay(i), tile_of(i) // 2, 0))
+
+    def whole(n_rows, width):
+        return pl.BlockSpec((1, n_rows, width), lambda i: (lay(i), 0, 0))
+
+    in_specs = [tile(rd), full(ff), tile(rf), full(d_model), full(n_w), full(d_model), full(nq), full(d_model)]
+    operands = list(ops)
+    any_spec = pl.BlockSpec(memory_space=pl.ANY)
+    out_shape = [jax.ShapeDtypeStruct((n_layers, r, w), F32)
+                 for r, w in ((d_model, ff), (ff, d_model), (nq, d_model), (nkv, d_model), (nkv, d_model), (nq, d_model))]
+    out_specs = [rows(rd, ff), rows(rf, d_model), half(128, d_model), whole(nkv, d_model), whole(nkv, d_model),
+                 half(128, d_model)]
+    scratch = []
+    if acts is not None:
+        operands += list(acts)
+        in_specs += [any_spec] * 4
+    aliases = {}
+    if prev is not None:
+        aliases = {len(operands) + i: i for i in range(6)}
+        operands += list(prev)
+        in_specs += [any_spec] * 6
+    if acts is not None:
+        seq = acts[0].shape[1]
+        out_shape += [jax.ShapeDtypeStruct((4, seq, d_model), F32)] * 4
+        out_specs += [any_spec] * 4
+        scratch = [pltpu.VMEM((4, 4, seq, d_model), F32), pltpu.SemaphoreType.DMA((4,)), pltpu.SemaphoreType.DMA((4, 4))]
     return pl.pallas_call(
-        ff_grad_kernel, grid=(n_layers, n_tiles),
-        out_shape=[jax.ShapeDtypeStruct((n_layers, d_model, ff), F32), jax.ShapeDtypeStruct((n_layers, ff, d_model), F32)],
-        in_specs=[pl.BlockSpec((1, tokens, rd), lambda l, t: (l, 0, t)), pl.BlockSpec((1, tokens, ff), lambda l, t: (l, 0, 0)),
-                  pl.BlockSpec((1, tokens, rf), lambda l, t: (l, 0, t)), pl.BlockSpec((1, tokens, d_model), lambda l, t: (l, 0, 0))],
-        out_specs=[pl.BlockSpec((1, rd, ff), lambda l, t: (l, t, 0)), pl.BlockSpec((1, rf, d_model), lambda l, t: (l, t, 0))],
-        compiler_params=pltpu.CompilerParams(dimension_semantics=("arbitrary", "arbitrary")),
-        cost_estimate=pl.CostEstimate(flops=30 * 10 ** 9, bytes_accessed=10 ** 8, transcendentals=0),
-        name="ff_grads",
-    )(n1, u, h, e)
-
-
-def attn_grad_kernel(dqkv_ref, n2_ref, a_ref, c_ref, dq_ref, dk_ref, dv_ref, do_ref, *, nq, nkv):
-    n2 = n2_ref[0]
-    dq_ref[0] = dot_tn(dqkv_ref[0, :, :nq], n2)
-    dk_ref[0] = dot_tn(dqkv_ref[0, :, nq:nq + nkv], n2)
-    dv_ref[0] = dot_tn(dqkv_ref[0, :, nq + nkv:], n2)
-    do_ref[0] = dot_tn(a_ref[0], c_ref[0])
-
-
-def attn_grads(dqkv, n2, a, c, nq, nkv):
-    n_layers, tokens, d_model = n2.shape
-    n_tiles = 2
-    cw = d_model // n_tiles
-    n_w = nq + 2 * nkv
-    return pl.pallas_call(
-        functools.partial(attn_grad_kernel, nq=nq, nkv=nkv), grid=(n_layers, n_tiles),
-        out_shape=[jax.ShapeDtypeStruct((n_layers, r, d_model), F32) for r in (nq, nkv, nkv, nq)],
-        in_specs=[pl.BlockSpec((1, tokens, n_w), lambda l, t: (l, 0, 0)), pl.BlockSpec((1, tokens, cw), lambda l, t: (l, 0, t)),
-                  pl.BlockSpec((1, tokens, nq), lambda l, t: (l, 0, 0)), pl.BlockSpec((1, tokens, cw), lambda l, t: (l, 0, t))],
-        out_specs=[pl.BlockSpec((1, r, cw), lambda l, t: (l, 0, t)) for r in (nq, nkv, nkv, nq)],
-        compiler_params=pltpu.CompilerParams(dimension_semantics=("arbitrary", "arbitrary")),
-        cost_estimate=pl.CostEstimate(flops=10 * 10 ** 9, bytes_accessed=3 * 10 ** 7, transcendentals=0),
-        name="attn_grads",
-    )(dqkv, n2, a, c)
-
-
-def gather_tp(own):
-    me = lax.axis_index("tp")
-    across = lax.ppermute(own, "tp", [(0, 2), (2, 0), (1, 3), (3, 1)])
-    chip = jnp.stack([own, across])
-    other = lax.ppermute(chip, "tp", [(0, 1), (1, 0), (2, 3), (3, 2)])
-    own_chip = jnp.where(me < 2, chip, chip[::-1])
-    oth_chip = jnp.where(me < 2, other, other[::-1])
-    even = lax.rem(me, 2) == 0
-    first = jnp.where(even, own_chip, oth_chip)
-    second = jnp.where(even, oth_chip, own_chip)
-    return [jnp.stack([first[0, i], second[0, i], first[1, i], second[1, i]]) for i in range(4)]
+        functools.partial(grad_kernel, nq=nq, nkv=nkv, n_tiles=n_tiles, start=start,
+                          n_prev=6 if prev is not None else 0, has_acts=acts is not None),
+        grid=(count,), out_shape=out_shape, in_specs=in_specs, out_specs=out_specs, scratch_shapes=scratch,
+        input_output_aliases=aliases,
+        compiler_params=pltpu.CompilerParams(dimension_semantics=("arbitrary",)),
+        cost_estimate=pl.CostEstimate(flops=10 ** 9 * count, bytes_accessed=6 * 10 ** 6 * count, transcendentals=0),
+        name="weight_grads",
+    )(*operands)
 
 
 def solution(mesh):
@@ -507,10 +591,21 @@
         n1, h, u, e, n2, a, c, dqkv, fin = run_chain(
             seq_lens, *acts, w_up, w_down, to_rows(w_query, nq), to_rows(w_key, nkv), to_rows(w_value, nkv),
             w_out.reshape(n_layers, nq, d_model))
-        gathered = gather_tp(fin)
-        d_up, d_down = ff_grads(n1, u, h, e)
-        dq, dk, dv, do = attn_grads(dqkv, n2, a, c, nq, nkv)
-        outs = gathered
+        ops = (n1, u, h, e, dqkv, n2, a, c)
+        across = lax.ppermute(fin, "tp", [(0, 2), (2, 0), (1, 3), (3, 1)])
+        cores = [(0, 1), (1, 0), (2, 3), (3, 2)]
+        near = lax.ppermute(fin, "tp", cores)
+        n_steps = n_layers * (2 * nq // 128)
+        cut_a = n_steps // 2
+        cut_b = cut_a + 4
+        grads = weight_grads(ops, 0, cut_a, nq, nkv)
+        across, dk = lax.optimization_barrier((across, grads[3]))
+        grads = list(grads[:3]) + [dk] + list(grads[4:])
+        far = lax.ppermute(across, "tp", cores)
+        grads = weight_grads(ops, cut_a, cut_b - cut_a, nq, nkv, prev=grads)
+        res = weight_grads(ops, cut_b, n_steps - cut_b, nq, nkv, prev=grads, acts=(fin, across, near, far))
+        d_up, d_down, dq, dk, dv, do = res[:6]
+        outs = [o.reshape(y_one.shape) for o in res[6:]]
         return (outs[0], outs[1], outs[2], outs[3],
                 from_rows(dq, heads), from_rows(dk, slots), from_rows(dv, slots),
                 do.reshape(n_layers, heads, head_dim, d_model), d_up, d_down)

time: 231 us -> 201 us (0.87)
  Pallas kernels: 208 us -> 195 us
  waiting for transfers between devices: 11.2 us -> 0.01 us
  other arithmetic: 8.4 us -> 0 us
    pallas_call x1, Pallas kernels: 161 us -> 133 us  [run_chain(): pl.pallas_call(body, out_shape=out_shape, in_specs=[pl.BlockSpec(memory_s...]
    pallas_call x2 -> x3, Pallas kernels: 47.3 us -> 62.4 us  [weight_grads(): pl.pallas_call(functools.partial(grad_kernel, nq=nq, nkv=nkv, n_tiles=n_t...]
    ppermute x2 -> x3, waiting for transfers between devices: 11.2 us -> 0.01 us  [the longest x1 0.01 us: local_fn(): across = lax.ppermute(fin, 'tp', [(0, 2), (2, 0), (1, 3), (3, 1)])]
    another operation x5 -> x0, other arithmetic: 5.57 us -> none  [the longest x4 4.17 us: gather_tp(): jnp.stack([first[0, i], second[0, i], first[1, i], second[1, i]])]
    select_n x1 -> x0, other arithmetic: 2.84 us -> none  [gather_tp(): first = jnp.where(even, own_chip, oth_chip)]
  transfers between devices with their start and end apart: 2 -> 3, of which waited for: 1 -> 0; matrix products, arithmetic and copies ran while one was open for 0% -> 0% of each run, Pallas kernels for 21% -> 20%
where the time goes in v2:
time: 201 us; the launch traced here: 200 us
  Pallas kernels  195 us (97%)
  starting transfers between devices  2.71 us (1%)
    pallas_call x1, Pallas kernels, run_chain(): pl.pallas_call(body, out_shape=out_shape, in_specs=[pl.BlockSpec(memory_s...  133 us
    pallas_call x3, Pallas kernels, weight_grads(): pl.pallas_call(functools.partial(grad_kernel, nq=nq, nkv=nkv, n_tiles=n_t...  62.4 us
  transfers between devices with their start and end apart: 3, of which 0 were waited for; matrix products, arithmetic and copies ran while one was open for 0% of the time, Pallas kernels for 20%

profile of v2, /device:TPU:0, one launch (start us, length us, event | category | flops | bytes accessed | tf_op | source)
XLA Modules:
  0.0 200.3 jit_solution(6204472437029814418)
XLA Ops:
  0.6 132.9 %chain.1 = (bf16[3,128,2048]{2,1,0:T(8,128)(2,1)}, bf16[3,128,2048]{2,1,0:T(8,128)(2,1)}, bf16[3,128,2048]{2,1,0:T(8,128)(2,1)}, bf16[3,128,2048]{2,1,0:T(8,128)...) custom-call(s32[4]{0:T(128)} %lens_ref.1, ...), custom_call_target="tpu_custom_call" | custom-call | flops 60000002048 | bytes 100000000 | tf_op jit(solution)/shard_map/chain/pallas_call | solution.py:436
  133.5 0.0 collective-permute-start.1
  133.5 2.5 %collective-permute-start = (f32[4,32,2048]{2,1,0:T(8,128)}, f32[4,32,2048]{2,1,0:T(8,128)S(1)}, u32[]{:S(2)}, u32[]{:S(2)}) collective-permute-start(f32[4,32,2048]{2,1,0:T(8,128)} %get-tuple-element.51.refs_8_), channel_id=1, source_target_pairs={{0,2},{2,0},{1,3},{3,1},{4,6},{6,4},{5,7},{7,5}} | collective-permute-start | bytes 3145736 | tf_op jit(solution)/shard_map/ppermute | solution.py:595
  136.0 27.6 %weight_grads.3 = (f32[3,2048,2048]{2,1,0:T(8,128)}, f32[3,2048,2048]{2,1,0:T(8,128)}, f32[3,512,2048]{2,1,0:T(8,128)}, f32[3,128,2048]{2,1,0:T(8,128)}, f32[3,1...) custom-call(bf16[3,128,2048]{2,1,0:T(8,128)(2,1)} %get-tuple-element.43.refs_0_, ...), custom_call_target="tpu_custom_call" | custom-call | flops 12000000000 | bytes 72000000 | tf_op jit(solution)/shard_map/weight_grads/pallas_call | solution.py:560
  163.6 0.0 collective-permute-done.refs_9_
  163.6 0.0 copy-start.1
  163.6 0.2 collective-permute-start.2
  163.9 11.6 %weight_grads.4 = (f32[3,2048,2048]{2,1,0:T(8,128)}, f32[3,2048,2048]{2,1,0:T(8,128)}, f32[3,512,2048]{2,1,0:T(8,128)}, f32[3,128,2048]{2,1,0:T(8,128)}, f32[3,1...) custom-call(bf16[3,128,2048]{2,1,0:T(8,128)(2,1)} %get-tuple-element, ...), custom_call_target="tpu_custom_call", output_to_operand_aliasing={{0}: (8, {}), {1}: (9, {}), {2}: (10, {}), {3}: (11, {}), {... | custom-call | flops 4000000000 | bytes 24000000 | tf_op jit(solution)/shard_map/weight_grads/pallas_call | solution.py:560
  175.5 0.0 copy-done.1
  175.5 0.0 collective-permute-done.1.refs_10_
  175.5 0.0 copy-start
  175.5 0.0 collective-permute-done.2.refs_11_
  175.5 0.0 copy-start.2
  175.5 1.0 copy-done
  176.5 0.4 copy-done.2
  176.9 23.2 %weight_grads.5 = (f32[3,2048,2048]{2,1,0:T(8,128)}, f32[3,2048,2048]{2,1,0:T(8,128)}, f32[3,512,2048]{2,1,0:T(8,128)}, f32[3,128,2048]{2,1,0:T(8,128)}, f32[3,1...) custom-call(bf16[3,128,2048]{2,1,0:T(8,128)(2,1)} %get-tuple-element, ...), custom_call_target="tpu_custom_call", output_to_operand_aliasing={{0}: (12, {}), {1}: (13, {}), {2}: (14, {}), {3}: (15, {}),... | custom-call | flops 8000000000 | bytes 48000000 | tf_op jit(solution)/shard_map/weight_grads/pallas_call | solution.py:560
Async XLA Ops:
  133.5 42.0 %collective-permute-start.1 = (f32[4,32,2048]{2,1,0:T(8,128)}, f32[4,32,2048]{2,1,0:T(8,128)S(1)}, u32[]{:S(2)}, u32[]{:S(2)}) collective-permute-start(f32[4,32,2048]{2,1,0:T(8,128)} %get-tuple-element.51.refs_8_), channel_id=1, source_target_pairs={{0,1},{1,0},{2,3},{3,2},{4,5},{5,4},{6,7},{7,6}} | collective-permute-start | bytes 3145736 | tf_op jit(solution)/shard_map/ppermute | solution.py:597
  133.5 30.1 %collective-permute-start = (f32[4,32,2048]{2,1,0:T(8,128)}, f32[4,32,2048]{2,1,0:T(8,128)S(1)}, u32[]{:S(2)}, u32[]{:S(2)}) collective-permute-start(f32[4,32,2048]{2,1,0:T(8,128)} %get-tuple-element.51.refs_8_), channel_id=1, source_target_pairs={{0,2},{2,0},{1,3},{3,1},{4,6},{6,4},{5,7},{7,5}} | collective-permute-start | bytes 3145736 | tf_op jit(solution)/shard_map/ppermute | solution.py:595
  163.6 11.9 %copy-start.1 = (f32[4,32,2048]{2,1,0:T(8,128)}, f32[4,32,2048]{2,1,0:T(8,128)S(1)}, u32[]{:S(2)}) copy-start(f32[4,32,2048]{2,1,0:T(8,128)S(1)} %collective-permute-done.refs_9_) | copy-start | bytes 3145732
  163.6 11.9 %collective-permute-start.2 = (f32[4,32,2048]{2,1,0:T(8,128)S(1)}, f32[4,32,2048]{2,1,0:T(8,128)S(1)}, u32[]{:S(2)}, u32[]{:S(2)}) collective-permute-start(f32[4,32,2048]{2,1,0:T(8,128)S(1)} %collective-permute-done.refs_9_), channel_id=1, source_target_pairs={{0,1},{1,0},{2,3},{3,2},{4,5},{5,4},{6,7},{7,6}} | collective-permute-start | bytes 3145736 | tf_op jit(solution)/shard_map/ppermute | solution.py:604
  175.5 1.0 copy-start
  175.5 1.4 copy-start.2

commit v3 on v2

--- a/solution.py
+++ b/solution.py
@@ -42,7 +42,7 @@
 
 
 def chain_kernel(lens_ref, y1_ref, y2_ref, d1_ref, d2_ref, wup_ref, wdn_ref, wq_ref, wk_ref, wv_ref, wo_ref,
-                 on1, oh, ou, oe, on2, oa, oc, odqkv, ofin,
+                 on1, oh, ou, oe, on2, oa, oc, odqkv, o_early, o_base, o_send, o_own,
                  w1, w2, wa, wo, n1b, eb, n2b, cb, hb, ub, ab, dqb, gp, qkv, pbuf,
                  part, rd, sx, rx, st,
                  s_in, s_w, s_out, s_ds, s_dr, s_xs, s_xr, s_as, s_ar, s_fin,
@@ -103,10 +103,15 @@
         part[ty, :, :, :, cols(k)] = val.reshape(2, 2, seq, cw)
         d_copy(ty, k).start()
 
-    def mid(ty, k):
+    def mid(ty, k, send=None):
         d_copy(ty, k).wait_recv()
         sx[ty, :, cols(k)] = part[ty, xo, ci, :, cols(k)] + rd[ty, xo, :, cols(k)]
-        x_copy(ty, k).start()
+        if send is None:
+            x_copy(ty, k).start()
+        else:
+            @pl.when(send)
+            def _():
+                x_copy(ty, k).start()
 
     def fin_sum(ty):
         for k in range(n_chunk):
@@ -252,32 +257,30 @@
         put_part(DW, k, dot_nn(dqb[lay], wa[:, cols(k)]))
 
     def g_fin(lay):
-        x2 = st[1] - fin_sum(G)
-        st[1] = x2
+        x2 = st[2] - fin_sum(G)
+        st[2] = x2
         ag_start(G, lay, (x2 * inv_rms(x2)).astype(BF16))
 
     def b_fin(lay):
-        dy1 = st[2] + rms_back(st[0], fin_sum(B))
-        st[2] = dy1
+        dy1 = st[3] + rms_back(st[0], fin_sum(B))
+        st[3] = dy1
         ag_start(B, lay, dy1.astype(BF16))
 
-    def f_fin(lay, more):
+    def f_fin(lay):
         x1 = st[0] - fin_sum(FW)
         st[0] = x1
-        if more:
-            ag_start(FW, lay - 1, (x1 * inv_rms(x1)).astype(BF16))
-
-    def d_fin(lay, more):
-        dx2 = st[3] + rms_back(st[1], fin_sum(DW))
-        st[3] = dx2
-        if more:
-            ag_start(DW, lay - 1, dx2.astype(BF16))
+        ag_start(FW, lay - 1, (x1 * inv_rms(x1)).astype(BF16))
+
+    def d_fin(lay):
+        dx2 = st[1] + rms_back(st[2], fin_sum(DW))
+        st[1] = dx2
+        ag_start(DW, lay - 1, dx2.astype(BF16))
 
     top = n_layers - 1
     in_full = [pltpu.make_async_copy(y1_ref, part.at[FW], s_in.at[0]),
                pltpu.make_async_copy(d2_ref, part.at[DW], s_in.at[1])]
     in_own = [pltpu.make_async_copy(src.at[xi, ci], st.at[i], s_in.at[2 + i])
-              for i, src in enumerate((y1_ref, y2_ref, d1_ref, d2_ref))]
+              for i, src in enumerate((y1_ref, d2_ref, y2_ref, d1_ref))]
     in_full[0].start()
     for k in range(2 * n_chunk):
         w_start(top, k)
@@ -304,8 +307,8 @@
 
         @pl.when(later)
         def _():
-            f_fin(lay + 1, True)
-            d_fin(lay + 1, True)
+            f_fin(lay + 1)
+            d_fin(lay + 1)
             ag_forward(FW, lay)
             ag_ready(FW, lay)
 
@@ -372,11 +375,11 @@
         f_put(lay, 1)
         f_put(lay, 2)
         f_put(lay, 3)
-        mid(FW, 0)
-        mid(FW, 1)
+        mid(FW, 0, more)
+        mid(FW, 1, more)
         ag_forward(B, lay)
-        mid(FW, 2)
-        mid(FW, 3)
+        mid(FW, 2, more)
+        mid(FW, 3, more)
         ag_ready(B, lay)
         out_copy(6, lay).start()
         d_attn(lay)
@@ -390,18 +393,25 @@
             w_start(lay - 1, W_OUT)
 
         for k in range(n_chunk):
-            mid(DW, k)
+            mid(DW, k, more)
         return carry
 
     lax.fori_loop(0, n_layers, layer_body, 0)
-    f_fin(0, False)
-    d_fin(0, False)
-    fin = pltpu.make_async_copy(st, ofin, s_fin)
-    fin.start()
+    for ty in (FW, DW):
+        rx[ty] = part[ty, xi, ci] + rd[ty, xi]
+    tail = [pltpu.make_async_copy(src, dst, s_fin.at[i]) for i, (src, dst) in enumerate(
+        ((st.at[pl.ds(2, 2)], o_early), (st.at[pl.ds(0, 2)], o_base),
+         (sx.at[pl.ds(FW, 2)], o_send), (rx.at[pl.ds(FW, 2)], o_own)))]
+    for cp in tail:
+        cp.start()
+    for ty in (FW, DW):
+        for k in range(n_chunk):
+            d_copy(ty, k).wait_send()
     for idx in range(8):
         for lay in range(n_layers):
             out_copy(idx, lay).wait()
-    fin.wait()
+    for cp in tail:
+        cp.wait()
 
 
 def run_chain(lens, y1, y2, d1, d2, w_up, w_down, wq, wk, wv, wo):
@@ -419,7 +429,7 @@
     wide_ff = jax.ShapeDtypeStruct((n_layers, tokens, ff), BF16)
     out_shape = [wide, wide_ff, wide_ff, wide, wide, jax.ShapeDtypeStruct((n_layers, tokens, nq), BF16), wide,
                  jax.ShapeDtypeStruct((n_layers, tokens, n_w), BF16),
-                 jax.ShapeDtypeStruct((4, seq, d_model), F32)]
+                 ] + [jax.ShapeDtypeStruct((2, seq, d_model), F32)] * 4
     vm = pltpu.VMEM
     dma = pltpu.SemaphoreType.DMA
     scratch = [vm((d_model, ff), BF16), vm((ff, d_model), BF16), vm((n_w, d_model), BF16), vm((nq, d_model), BF16),
@@ -432,11 +442,11 @@
                vm((4, seq, d_model), F32), vm((4, seq, d_model), F32), vm((4, seq, d_model), F32),
                dma((6,)), dma((2 * n_chunk + 4,)), dma((8, n_layers)),
                dma((4, n_chunk)), dma((4, n_chunk)), dma((4, n_chunk)), dma((4, n_chunk)),
-               dma((4, 3)), dma((4, 3)), dma]
+               dma((4, 3)), dma((4, 3)), dma((4,))]
     return pl.pallas_call(
         body, out_shape=out_shape,
         in_specs=[pl.BlockSpec(memory_space=pltpu.SMEM)] + [any_spec] * 10,
-        out_specs=[any_spec] * 9,
+        out_specs=[any_spec] * 12,
         scratch_shapes=scratch,
         compiler_params=pltpu.CompilerParams(collective_id=0, has_side_effects=True, vmem_limit_bytes=60 * 2 ** 20),
         cost_estimate=pl.CostEstimate(flops=60 * 10 ** 9, bytes_accessed=10 ** 8, transcendentals=0),
@@ -444,15 +454,10 @@
     )(lens, y1, y2, d1, d2, w_up, w_down, wq, wk, wv, wo)
 
 
-def grad_kernel(*refs, nq, nkv, n_tiles, start, n_prev, has_acts):
+def grad_kernel(*refs, nq, nkv, n_tiles, start, n_prev):
     n1_ref, u_ref, h_ref, e_ref, dqkv_ref, n2_ref, a_ref, c_ref = refs[:8]
-    pos = 8
-    if has_acts:
-        srcs = refs[pos:pos + 4]
-        pos += 4
-    pos += n_prev
+    pos = 8 + n_prev
     dup_ref, ddn_ref, dq_ref, dk_ref, dv_ref, do_ref = refs[pos:pos + 6]
-    pos += 6
     idx = pl.program_id(0)
     step = lax.rem(idx + start, n_tiles)
     dup_ref[0] = dot_tn(n1_ref[0], u_ref[0])
@@ -475,39 +480,8 @@
     def _():
         dv_ref[0] = dot_tn(dqkv_ref[0, :, nq + nkv:], n2_ref[0])
 
-    if has_acts:
-        out_refs = refs[pos:pos + 4]
-        buf, s_ld, s_st = refs[pos + 4:]
-        me = lax.axis_index("tp")
-        xi, ci = lax.div(me, 2), lax.rem(me, 2)
-        slots = (me, 2 * (1 - xi) + ci, 2 * xi + 1 - ci, 2 * (1 - xi) + 1 - ci)
-
-        def load(i):
-            return pltpu.make_async_copy(srcs[i], buf.at[i], s_ld.at[i])
-
-        def store(i, j):
-            return pltpu.make_async_copy(buf.at[i, j], out_refs[j].at[slots[i]], s_st.at[i, j])
-
-        @pl.when(idx == 0)
-        def _():
-            for i in range(4):
-                load(i).start()
-
-        @pl.when(idx == 2)
-        def _():
-            for i in range(4):
-                load(i).wait()
-                for j in range(4):
-                    store(i, j).start()
-
-        @pl.when(idx == 5)
-        def _():
-            for i in range(4):
-                for j in range(4):
-                    store(i, j).wait()
-
-
-def weight_grads(ops, start, count, nq, nkv, prev=None, acts=None):
+
+def weight_grads(ops, start, count, nq, nkv, prev=None):
     n1, u, h, e, dqkv, n2, a, c = ops
     n_layers, tokens, d_model = n1.shape
     ff = u.shape[2]
@@ -543,29 +517,58 @@
                  for r, w in ((d_model, ff), (ff, d_model), (nq, d_model), (nkv, d_model), (nkv, d_model), (nq, d_model))]
     out_specs = [rows(rd, ff), rows(rf, d_model), half(128, d_model), whole(nkv, d_model), whole(nkv, d_model),
                  half(128, d_model)]
-    scratch = []
-    if acts is not None:
-        operands += list(acts)
-        in_specs += [any_spec] * 4
     aliases = {}
     if prev is not None:
         aliases = {len(operands) + i: i for i in range(6)}
         operands += list(prev)
         in_specs += [any_spec] * 6
-    if acts is not None:
-        seq = acts[0].shape[1]
-        out_shape += [jax.ShapeDtypeStruct((4, seq, d_model), F32)] * 4
-        out_specs += [any_spec] * 4
-        scratch = [pltpu.VMEM((4, 4, seq, d_model), F32), pltpu.SemaphoreType.DMA((4,)), pltpu.SemaphoreType.DMA((4, 4))]
     return pl.pallas_call(
         functools.partial(grad_kernel, nq=nq, nkv=nkv, n_tiles=n_tiles, start=start,
-                          n_prev=6 if prev is not None else 0, has_acts=acts is not None),
-        grid=(count,), out_shape=out_shape, in_specs=in_specs, out_specs=out_specs, scratch_shapes=scratch,
+                          n_prev=6 if prev is not None else 0),
+        grid=(count,), out_shape=out_shape, in_specs=in_specs, out_specs=out_specs,
         input_output_aliases=aliases,
         compiler_params=pltpu.CompilerParams(dimension_semantics=("arbitrary",)),
         cost_estimate=pl.CostEstimate(flops=10 ** 9 * count, bytes_accessed=6 * 10 ** 6 * count, transcendentals=0),
         name="weight_grads",
     )(*operands)
+
+
+def last_kernel(base_ref, early_ref, own_ref, got_ref, late_ref):
+    late_ref[0] = base_ref[0] - (own_ref[0] + got_ref[0])
+    late_ref[1] = base_ref[1] + rms_back(early_ref[0], own_ref[1] + got_ref[1])
+
+
+def last_sums(base, early, own, got):
+    vmem = pl.BlockSpec(memory_space=pltpu.VMEM)
+    return pl.pallas_call(
+        last_kernel, out_shape=jax.ShapeDtypeStruct(base.shape, F32), in_specs=[vmem] * 4, out_specs=vmem,
+        compiler_params=pltpu.CompilerParams(vmem_limit_bytes=8 * 2 ** 20), name="last_sums",
+    )(base, early, own, got)
+
+
+def place_kernel(*refs):
+    early, late, out_refs, sems = refs[:4], refs[4:8], refs[8:12], refs[12]
+    me = lax.axis_index("tp")
+    xi, ci = lax.div(me, 2), lax.rem(me, 2)
+    slots = (me, 2 * (1 - xi) + ci, 2 * xi + 1 - ci, 2 * (1 - xi) + 1 - ci)
+    copies = []
+    for i in range(4):
+        for j, src in enumerate((late[i].at[0], early[i].at[0], early[i].at[1], late[i].at[1])):
+            copies.append(pltpu.make_async_copy(src, out_refs[j].at[slots[i]], sems.at[i, j]))
+    for cp in copies:
+        cp.start()
+    for cp in copies:
+        cp.wait()
+
+
+def place(early, late):
+    _, seq, d_model = early[0].shape
+    return pl.pallas_call(
+        place_kernel, out_shape=[jax.ShapeDtypeStruct((4, seq, d_model), F32)] * 4,
+        in_specs=[pl.BlockSpec(memory_space=pltpu.VMEM)] * 8, out_specs=[pl.BlockSpec(memory_space=pl.ANY)] * 4,
+        scratch_shapes=[pltpu.SemaphoreType.DMA((4, 4))],
+        compiler_params=pltpu.CompilerParams(vmem_limit_bytes=16 * 2 ** 20), name="place",
+    )(*early, *late)
 
 
 def solution(mesh):
@@ -588,24 +591,34 @@
             return jnp.transpose(g.reshape(n_layers, n_heads, head_dim, d_model), (0, 3, 1, 2))
 
         acts = [a.reshape(2, 2, seq, d_model) for a in (y_one, y_two, dy_one, dy_two)]
-        n1, h, u, e, n2, a, c, dqkv, fin = run_chain(
+        n1, h, u, e, n2, a, c, dqkv, early, base, send, own = run_chain(
             seq_lens, *acts, w_up, w_down, to_rows(w_query, nq), to_rows(w_key, nkv), to_rows(w_value, nkv),
             w_out.reshape(n_layers, nq, d_model))
         ops = (n1, u, h, e, dqkv, n2, a, c)
-        across = lax.ppermute(fin, "tp", [(0, 2), (2, 0), (1, 3), (3, 1)])
+        chips = [(0, 2), (2, 0), (1, 3), (3, 1)]
         cores = [(0, 1), (1, 0), (2, 3), (3, 2)]
-        near = lax.ppermute(fin, "tp", cores)
+        got = lax.ppermute(send, "tp", chips)
+        early_c = lax.ppermute(early, "tp", cores)
         n_steps = n_layers * (2 * nq // 128)
-        cut_a = n_steps // 2
-        cut_b = cut_a + 4
-        grads = weight_grads(ops, 0, cut_a, nq, nkv)
-        across, dk = lax.optimization_barrier((across, grads[3]))
-        grads = list(grads[:3]) + [dk] + list(grads[4:])
-        far = lax.ppermute(across, "tp", cores)
-        grads = weight_grads(ops, cut_a, cut_b - cut_a, nq, nkv, prev=grads)
-        res = weight_grads(ops, cut_b, n_steps - cut_b, nq, nkv, prev=grads, acts=(fin, across, near, far))
-        d_up, d_down, dq, dk, dv, do = res[:6]
-        outs = [o.reshape(y_one.shape) for o in res[6:]]
+        cut = n_steps // 4
+
+        def tie(grads, *vals):
+            tied = lax.optimization_barrier((grads[3],) + vals)
+            return list(grads[:3]) + [tied[0]] + list(grads[4:]), tied[1:]
+
+        grads = weight_grads(ops, 0, cut, nq, nkv)
+        grads, (got, early) = tie(grads, got, early)
+        late = last_sums(base, early, own, got)
+        grads, (late,) = tie(grads, late)
+        late_x = lax.ppermute(late, "tp", chips)
+        early_x = lax.ppermute(early, "tp", chips)
+        late_c = lax.ppermute(late, "tp", cores)
+        grads = weight_grads(ops, cut, n_steps - cut, nq, nkv, prev=grads)
+        grads, (early_x, late_x) = tie(grads, early_x, late_x)
+        early_d = lax.ppermute(early_x, "tp", cores)
+        late_d = lax.ppermute(late_x, "tp", cores)
+        d_up, d_down, dq, dk, dv, do = grads
+        outs = [o.reshape(y_one.shape) for o in place((early, early_x, early_c, early_d), (late, late_x, late_c, late_d))]
         return (outs[0], outs[1], outs[2], outs[3],
                 from_rows(dq, heads), from_rows(dk, slots), from_rows(dv, slots),
                 do.reshape(n_layers, heads, head_dim, d_model), d_up, d_down)

time: 201 us -> 191 us (0.950)
  Pallas kernels: 195 us -> 185 us
  waiting for transfers between devices: 0.01 us -> 2.26 us
    pallas_call x3 -> x2, Pallas kernels: 62.4 us -> 55.1 us  [weight_grads(): pl.pallas_call(functools.partial(grad_kernel, nq=nq, nkv=nkv, n_tiles=n_t...]
    pallas_call x1, Pallas kernels: 133 us -> 126 us  [run_chain(): pl.pallas_call(body, out_shape=out_shape, in_specs=[pl.BlockSpec(memory_s...]
    pallas_call x0 -> x2, Pallas kernels: none -> 3.42 us  [the longest x1 3.17 us: place(): pl.pallas_call(place_kernel, out_shape=[jax.ShapeDtypeStruct((4, seq, d_m...]
    ppermute x3 -> x7, waiting for transfers between devices: 0.01 us -> 2.26 us  [the longest x1 1.5 us: local_fn(): early_d = lax.ppermute(early_x, 'tp', cores)]
  transfers between devices with their start and end apart: 3 -> 7, of which waited for: 0 -> 2; matrix products, arithmetic and copies ran while one was open for 0% -> 0% of each run, Pallas kernels for 20% -> 29%
where the time goes in v3:
time: 191 us
  Pallas kernels  185 us (97%)
  starting transfers between devices  3.29 us (2%)
  waiting for transfers between devices  2.26 us (1%)
    pallas_call x1, Pallas kernels, run_chain(): pl.pallas_call(body, out_shape=out_shape, in_specs=[pl.BlockSpec(memory_s...  126 us
    pallas_call x2, Pallas kernels, weight_grads(): pl.pallas_call(functools.partial(grad_kernel, nq=nq, nkv=nkv, n_tiles=n_t...  55.1 us
  transfers between devices with their start and end apart: 7, of which 2 were waited for; matrix products, arithmetic and copies ran while one was open for 0% of the time, Pallas kernels for 29%

profile of v3, /device:TPU:0, one launch (start us, length us, event | category | flops | bytes accessed | tf_op | source)
XLA Modules:
  0.0 191.0 jit_solution(9155285453223803444)
XLA Ops:
  0.6 126.0 %chain.1 = (bf16[3,128,2048]{2,1,0:T(8,128)(2,1)}, bf16[3,128,2048]{2,1,0:T(8,128)(2,1)}, bf16[3,128,2048]{2,1,0:T(8,128)(2,1)}, bf16[3,128,2048]{2,1,0:T(8,128)...) custom-call(s32[4]{0:T(128)} %lens_ref.1, ...), custom_call_target="tpu_custom_call" | custom-call | flops 60000002048 | bytes 100000000 | tf_op jit(solution)/shard_map/chain/pallas_call | solution.py:446
  126.7 0.7 collective-permute-start
  127.3 0.0 collective-permute-start.3
  127.3 0.0 copy-start
  127.3 0.0 copy-start.1
  127.3 0.0 copy-start.2
  127.3 15.7 %weight_grads.2 = (f32[3,2048,2048]{2,1,0:T(8,128)}, f32[3,2048,2048]{2,1,0:T(8,128)}, f32[3,512,2048]{2,1,0:T(8,128)}, f32[3,128,2048]{2,1,0:T(8,128)}, f32[3,1...) custom-call(bf16[3,128,2048]{2,1,0:T(8,128)(2,1)} %get-tuple-element.46.refs_0_, ...), custom_call_target="tpu_custom_call" | custom-call | flops 6000000000 | bytes 36000000 | tf_op jit(solution)/shard_map/weight_grads/pallas_call | solution.py:525
  143.0 0.0 collective-permute-done.got_ref
  143.0 0.0 copy-done
  143.0 1.5 collective-permute-start.1
  144.5 0.0 copy-done.1
  144.5 0.0 copy-done.2
  144.5 0.2 last_sums.1.refs_4_
  144.7 0.6 collective-permute-start.2
  145.4 0.0 collective-permute-start.5
  145.4 39.5 %weight_grads.3 = (f32[3,2048,2048]{2,1,0:T(8,128)}, f32[3,2048,2048]{2,1,0:T(8,128)}, f32[3,512,2048]{2,1,0:T(8,128)}, f32[3,128,2048]{2,1,0:T(8,128)}, f32[3,1...) custom-call(bf16[3,128,2048]{2,1,0:T(8,128)(2,1)} %get-tuple-element, ...), custom_call_target="tpu_custom_call", output_to_operand_aliasing={{0}: (8, {}), {1}: (9, {}), {2}: (10, {}), {3}: (11, {}), {... | custom-call | flops 17999998976 | bytes 108000000 | tf_op jit(solution)/shard_map/weight_grads/pallas_call | solution.py:525
  184.8 0.0 collective-permute-done.2.refs_5_
  184.8 0.0 collective-permute-done.1.refs_1_
  184.8 0.5 collective-permute-start.4
  185.4 0.0 collective-permute-start.6
  185.4 0.0 collective-permute-done.3.refs_2_
  185.4 0.0 collective-permute-done.5.refs_6_
  185.4 1.5 collective-permute-done.4.refs_3_
  186.9 0.7 collective-permute-done.6.refs_7_
  187.7 3.2 %place.1 = (f32[4,32,2048]{2,1,0:T(8,128)}, f32[4,32,2048]{2,1,0:T(8,128)}, f32[4,32,2048]{2,1,0:T(8,128)}, f32[4,32,2048]{2,1,0:T(8,128)}) custom-call(f32[2,32,2048]{2,1,0:T(8,128)S(1)} %copy-done, f32[2,32,2048]{2,1,0:T(8,128)} %collective-permute-done.1.refs_1_, f32[2,32,2048]{2,1,0:T(8,128)S(1)} %collective-permute-done.3.refs_2_, ...), custom_call_target="tpu_custom_call" | custom-call | tf_op jit(solution)/shard_map/place/pallas_call | solution.py:566
Async XLA Ops:
  126.7 16.4 %collective-permute-start = (f32[2,32,2048]{2,1,0:T(8,128)}, f32[2,32,2048]{2,1,0:T(8,128)S(1)}, u32[]{:S(2)}, u32[]{:S(2)}) collective-permute-start(f32[2,32,2048]{2,1,0:T(8,128)} %get-tuple-element.55), channel_id=1, source_target_pairs={{0,2},{2,0},{1,3},{3,1},{4,6},{6,4},{5,7},{7,5}} | collective-permute-start | bytes 1572872 | tf_op jit(solution)/shard_map/ppermute | solution.py:600
  127.3 58.1 %collective-permute-start.3 = (f32[2,32,2048]{2,1,0:T(8,128)}, f32[2,32,2048]{2,1,0:T(8,128)S(1)}, u32[]{:S(2)}, u32[]{:S(2)}) collective-permute-start(f32[2,32,2048]{2,1,0:T(8,128)} %get-tuple-element.57.early_ref.refs_0_), channel_id=1, source_target_pairs={{0,1},{1,0},{2,3},{3,2},{4,5},{5,4},{6,7},{7,6}} | collective-permute-start | bytes 1572872 | tf_op jit(solution)/shard_map/ppermute | solution.py:601
  127.3 15.7 %copy-start = (f32[2,32,2048]{2,1,0:T(8,128)S(1)}, f32[2,32,2048]{2,1,0:T(8,128)}, u32[]{:S(2)}) copy-start(f32[2,32,2048]{2,1,0:T(8,128)} %get-tuple-element.57.early_ref.refs_0_) | copy-start | bytes 1572868
  127.3 17.2 %copy-start.1 = (f32[2,32,2048]{2,1,0:T(8,128)S(1)}, f32[2,32,2048]{2,1,0:T(8,128)}, u32[]{:S(2)}) copy-start(f32[2,32,2048]{2,1,0:T(8,128)} %get-tuple-element.62.base_ref) | copy-start | bytes 1572868
  127.3 17.2 %copy-start.2 = (f32[2,32,2048]{2,1,0:T(8,128)S(1)}, f32[2,32,2048]{2,1,0:T(8,128)}, u32[]{:S(2)}) copy-start(f32[2,32,2048]{2,1,0:T(8,128)} %get-tuple-element.63.own_ref) | copy-start | bytes 1572868
  143.0 41.8 %collective-permute-start.1 = (f32[2,32,2048]{2,1,0:T(8,128)S(1)}, f32[2,32,2048]{2,1,0:T(8,128)}, u32[]{:S(2)}, u32[]{:S(2)}) collective-permute-start(f32[2,32,2048]{2,1,0:T(8,128)S(1)} %copy-done), channel_id=1, source_target_pairs={{0,2},{2,0},{1,3},{3,1},{4,6},{6,4},{5,7},{7,5}} | collective-permute-start | bytes 1572872 | tf_op jit(solution)/shard_map/ppermute | solution.py:614
  144.7 40.1 %collective-permute-start.2 = (f32[2,32,2048]{2,1,0:T(8,128)S(1)}, f32[2,32,2048]{2,1,0:T(8,128)S(1)}, u32[]{:S(2)}, u32[]{:S(2)}) collective-permute-start(f32[2,32,2048]{2,1,0:T(8,128)S(1)} %last_sums.1.refs_4_), channel_id=1, source_target_pairs={{0,2},{2,0},{1,3},{3,1},{4,6},{6,4},{5,7},{7,5}} | collective-permute-start | bytes 1572872 | tf_op jit(solution)/shard_map/ppermute | solution.py:613
  145.4 40.0 %collective-permute-start.5 = (f32[2,32,2048]{2,1,0:T(8,128)S(1)}, f32[2,32,2048]{2,1,0:T(8,128)S(1)}, u32[]{:S(2)}, u32[]{:S(2)}) collective-permute-start(f32[2,32,2048]{2,1,0:T(8,128)S(1)} %last_sums.1.refs_4_), channel_id=1, source_target_pairs={{0,1},{1,0},{2,3},{3,2},{4,5},{5,4},{6,7},{7,6}} | collective-permute-start | bytes 1572872 | tf_op jit(solution)/shard_map/ppermute | solution.py:615
  184.8 2.1 %collective-permute-start.4 = (f32[2,32,2048]{2,1,0:T(8,128)}, f32[2,32,2048]{2,1,0:T(8,128)S(1)}, u32[]{:S(2)}, u32[]{:S(2)}) collective-permute-start(f32[2,32,2048]{2,1,0:T(8,128)} %collective-permute-done.1.refs_1_), channel_id=1, source_target_pairs={{0,1},{1,0},{2,3},{3,2},{4,5},{5,4},{6,7},{7,6}} | collective-permute-start | bytes 1572872 | tf_op jit(solution)/shard_map/ppermute | solution.py:618
  185.4 2.3 %collective-permute-start.6 = (f32[2,32,2048]{2,1,0:T(8,128)S(1)}, f32[2,32,2048]{2,1,0:T(8,128)S(1)}, u32[]{:S(2)}, u32[]{:S(2)}) collective-permute-start(f32[2,32,2048]{2,1,0:T(8,128)S(1)} %collective-permute-done.2.refs_5_), channel_id=1, source_target_pairs={{0,1},{1,0},{2,3},{3,2},{4,5},{5,4},{6,7},{7,6}} | collective-permute-start | bytes 1572872 | tf_op jit(solution)/shard_map/ppermute | solution.py:619

commit v4 on v3

--- a/solution.py
+++ b/solution.py
@@ -359,8 +359,8 @@
                 w_start(lay - 1, k)
 
         mid(B, 1)
+        g_fin(lay)
         mid(B, 2)
-        g_fin(lay)
         mid(B, 3)
         ag_forward(G, lay)
         b_fin(lay)
@@ -472,11 +472,11 @@
     def _():
         do_ref[0] = dot_tn(a_ref[0, :, tile], c_ref[0])
 
-    @pl.when((step == 1) | (idx == 0))
+    @pl.when(step == 1)
     def _():
         dk_ref[0] = dot_tn(dqkv_ref[0, :, nq:nq + nkv], n2_ref[0])
 
-    @pl.when((step == 2) | (idx == 0))
+    @pl.when(step == 4)
     def _():
         dv_ref[0] = dot_tn(dqkv_ref[0, :, nq + nkv:], n2_ref[0])
 
@@ -533,42 +533,42 @@
     )(*operands)
 
 
-def last_kernel(base_ref, early_ref, own_ref, got_ref, late_ref):
-    late_ref[0] = base_ref[0] - (own_ref[0] + got_ref[0])
-    late_ref[1] = base_ref[1] + rms_back(early_ref[0], own_ref[1] + got_ref[1])
+def last_kernel(base_ref, early_ref, own_ref, got_ref, fin_ref):
+    fin_ref[0] = base_ref[0] - (own_ref[0] + got_ref[0])
+    fin_ref[1] = early_ref[0]
+    fin_ref[2] = early_ref[1]
+    fin_ref[3] = base_ref[1] + rms_back(early_ref[0], own_ref[1] + got_ref[1])
 
 
 def last_sums(base, early, own, got):
     vmem = pl.BlockSpec(memory_space=pltpu.VMEM)
     return pl.pallas_call(
-        last_kernel, out_shape=jax.ShapeDtypeStruct(base.shape, F32), in_specs=[vmem] * 4, out_specs=vmem,
+        last_kernel, out_shape=jax.ShapeDtypeStruct((4,) + base.shape[1:], F32), in_specs=[vmem] * 4, out_specs=vmem,
         compiler_params=pltpu.CompilerParams(vmem_limit_bytes=8 * 2 ** 20), name="last_sums",
     )(base, early, own, got)
 
 
 def place_kernel(*refs):
-    early, late, out_refs, sems = refs[:4], refs[4:8], refs[8:12], refs[12]
+    srcs, out_refs, sems = refs[:4], refs[4:8], refs[8]
     me = lax.axis_index("tp")
     xi, ci = lax.div(me, 2), lax.rem(me, 2)
     slots = (me, 2 * (1 - xi) + ci, 2 * xi + 1 - ci, 2 * (1 - xi) + 1 - ci)
-    copies = []
-    for i in range(4):
-        for j, src in enumerate((late[i].at[0], early[i].at[0], early[i].at[1], late[i].at[1])):
-            copies.append(pltpu.make_async_copy(src, out_refs[j].at[slots[i]], sems.at[i, j]))
+    copies = [pltpu.make_async_copy(srcs[i].at[j], out_refs[j].at[slots[i]], sems.at[i, j])
+              for i in range(4) for j in range(4)]
     for cp in copies:
         cp.start()
     for cp in copies:
         cp.wait()
 
 
-def place(early, late):
-    _, seq, d_model = early[0].shape
+def place(*parts):
+    _, seq, d_model = parts[0].shape
     return pl.pallas_call(
         place_kernel, out_shape=[jax.ShapeDtypeStruct((4, seq, d_model), F32)] * 4,
-        in_specs=[pl.BlockSpec(memory_space=pltpu.VMEM)] * 8, out_specs=[pl.BlockSpec(memory_space=pl.ANY)] * 4,
+        in_specs=[pl.BlockSpec(memory_space=pltpu.VMEM)] * 4, out_specs=[pl.BlockSpec(memory_space=pl.ANY)] * 4,
         scratch_shapes=[pltpu.SemaphoreType.DMA((4, 4))],
         compiler_params=pltpu.CompilerParams(vmem_limit_bytes=16 * 2 ** 20), name="place",
-    )(*early, *late)
+    )(*parts)
 
 
 def solution(mesh):
@@ -598,27 +598,23 @@
         chips = [(0, 2), (2, 0), (1, 3), (3, 1)]
         cores = [(0, 1), (1, 0), (2, 3), (3, 2)]
         got = lax.ppermute(send, "tp", chips)
-        early_c = lax.ppermute(early, "tp", cores)
-        n_steps = n_layers * (2 * nq // 128)
-        cut = n_steps // 4
+        n_tiles = 2 * nq // 128
 
         def tie(grads, *vals):
             tied = lax.optimization_barrier((grads[3],) + vals)
             return list(grads[:3]) + [tied[0]] + list(grads[4:]), tied[1:]
 
-        grads = weight_grads(ops, 0, cut, nq, nkv)
-        grads, (got, early) = tie(grads, got, early)
-        late = last_sums(base, early, own, got)
-        grads, (late,) = tie(grads, late)
-        late_x = lax.ppermute(late, "tp", chips)
-        early_x = lax.ppermute(early, "tp", chips)
-        late_c = lax.ppermute(late, "tp", cores)
-        grads = weight_grads(ops, cut, n_steps - cut, nq, nkv, prev=grads)
-        grads, (early_x, late_x) = tie(grads, early_x, late_x)
-        early_d = lax.ppermute(early_x, "tp", cores)
-        late_d = lax.ppermute(late_x, "tp", cores)
+        grads = weight_grads(ops, 0, n_tiles, nq, nkv)
+        grads, (got,) = tie(grads, got)
+        fin = last_sums(base, early, own, got)
+        grads, (fin,) = tie(grads, fin)
+        across = lax.ppermute(fin, "tp", chips)
+        near = lax.ppermute(fin, "tp", cores)
+        grads = weight_grads(ops, n_tiles, (n_layers - 1) * n_tiles, nq, nkv, prev=grads)
+        grads, (across,) = tie(grads, across)
+        far = lax.ppermute(across, "tp", cores)
         d_up, d_down, dq, dk, dv, do = grads
-        outs = [o.reshape(y_one.shape) for o in place((early, early_x, early_c, early_d), (late, late_x, late_c, late_d))]
+        outs = [o.reshape(y_one.shape) for o in place(fin, across, near, far)]
         return (outs[0], outs[1], outs[2], outs[3],
                 from_rows(dq, heads), from_rows(dk, slots), from_rows(dv, slots),
                 do.reshape(n_layers, heads, head_dim, d_model), d_up, d_down)

time: 191 us -> 187 us (0.979)
  Pallas kernels: 185 us -> 181 us
    pallas_call x2, Pallas kernels: 55.1 us -> 52.7 us  [weight_grads(): pl.pallas_call(functools.partial(grad_kernel, nq=nq, nkv=nkv, n_tiles=n_t...]
  transfers between devices with their start and end apart: 7 -> 4, of which waited for: 2 -> 1; matrix products, arithmetic and copies ran while one was open for 0% -> 0% of each run, Pallas kernels for 29% -> 28%
where the time goes in v4:
time: 187 us; the launch traced here: 186 us
  Pallas kernels  181 us (97%)
  waiting for transfers between devices  2.53 us (1%)
  starting transfers between devices  2.3 us (1%)
    pallas_call x1, Pallas kernels, run_chain(): pl.pallas_call(body, out_shape=out_shape, in_specs=[pl.BlockSpec(memory_s...  126 us
    pallas_call x2, Pallas kernels, weight_grads(): pl.pallas_call(functools.partial(grad_kernel, nq=nq, nkv=nkv, n_tiles=n_t...  52.7 us
  transfers between devices with their start and end apart: 4, of which 1 were waited for; matrix products, arithmetic and copies ran while one was open for 0% of the time, Pallas kernels for 28%

profile of v4, /device:TPU:0, one launch (start us, length us, event | category | flops | bytes accessed | tf_op | source)
XLA Modules:
  0.0 186.4 jit_solution(17582785673407388978)
XLA Ops:
  0.6 125.6 %chain.1 = (bf16[3,128,2048]{2,1,0:T(8,128)(2,1)}, bf16[3,128,2048]{2,1,0:T(8,128)(2,1)}, bf16[3,128,2048]{2,1,0:T(8,128)(2,1)}, bf16[3,128,2048]{2,1,0:T(8,128)...) custom-call(s32[4]{0:T(128)} %lens_ref.1, ...), custom_call_target="tpu_custom_call" | custom-call | flops 60000002048 | bytes 100000000 | tf_op jit(solution)/shard_map/chain/pallas_call | solution.py:446
  126.3 0.7 collective-permute-start
  127.0 0.0 copy-start
  127.0 0.0 copy-start.1
  127.0 0.0 copy-start.2
  127.0 18.7 %weight_grads.2 = (f32[3,2048,2048]{2,1,0:T(8,128)}, f32[3,2048,2048]{2,1,0:T(8,128)}, f32[3,512,2048]{2,1,0:T(8,128)}, f32[3,128,2048]{2,1,0:T(8,128)}, f32[3,1...) custom-call(bf16[3,128,2048]{2,1,0:T(8,128)(2,1)} %get-tuple-element.44.refs_0_, ...), custom_call_target="tpu_custom_call" | custom-call | flops 8000000000 | bytes 48000000 | tf_op jit(solution)/shard_map/weight_grads/pallas_call | solution.py:525
  145.6 0.0 collective-permute-done.got_ref
  145.7 0.0 copy-done
  145.7 0.0 copy-done.1
  145.7 0.0 copy-done.2
  145.7 0.3 last_sums.1.refs_0_
  145.9 0.0 collective-permute-start.2
  146.0 1.4 collective-permute-start.1
  147.4 34.0 %weight_grads.3 = (f32[3,2048,2048]{2,1,0:T(8,128)}, f32[3,2048,2048]{2,1,0:T(8,128)}, f32[3,512,2048]{2,1,0:T(8,128)}, f32[3,128,2048]{2,1,0:T(8,128)}, f32[3,1...) custom-call(bf16[3,128,2048]{2,1,0:T(8,128)(2,1)} %get-tuple-element, ...), custom_call_target="tpu_custom_call", output_to_operand_aliasing={{0}: (8, {}), {1}: (9, {}), {2}: (10, {}), {3}: (11, {}), {... | custom-call | flops 16000000000 | bytes 96000000 | tf_op jit(solution)/shard_map/weight_grads/pallas_call | solution.py:525
  181.4 0.0 collective-permute-done.1.refs_1_
  181.4 0.2 collective-permute-start.3
  181.6 0.0 collective-permute-done.2.refs_2_
  181.6 2.5 %collective-permute-done.3.refs_3_ = f32[4,32,2048]{2,1,0:T(8,128)S(1)} collective-permute-done((f32[4,32,2048]{2,1,0:T(8,128)S(1)}, f32[4,32,2048]{2,1,0:T(8,128)S(1)}, u32[]{:S(2)}, u32[]{:S(2)}) %collective-permute-start.3) | collective-permute-done | bytes 1048608 | tf_op jit(solution)/shard_map/ppermute | solution.py:615
  184.1 2.1 %place.1 = (f32[4,32,2048]{2,1,0:T(8,128)}, f32[4,32,2048]{2,1,0:T(8,128)}, f32[4,32,2048]{2,1,0:T(8,128)}, f32[4,32,2048]{2,1,0:T(8,128)}) custom-call(f32[4,32,2048]{2,1,0:T(8,128)S(1)} %last_sums.1.refs_0_, f32[4,32,2048]{2,1,0:T(8,128)S(1)} %collective-permute-done.1.refs_1_, f32[4,32,2048]{2,1,0:T(8,128)S(1)} %collective-permute-done.2.refs_2_, ...), custom_call_target="tpu_custom_call" | custom-call | tf_op jit(solution)/shard_map/place/pallas_call | solution.py:566
Async XLA Ops:
  126.3 19.4 %collective-permute-start = (f32[2,32,2048]{2,1,0:T(8,128)}, f32[2,32,2048]{2,1,0:T(8,128)S(1)}, u32[]{:S(2)}, u32[]{:S(2)}) collective-permute-start(f32[2,32,2048]{2,1,0:T(8,128)} %get-tuple-element.53), channel_id=1, source_target_pairs={{0,2},{2,0},{1,3},{3,1},{4,6},{6,4},{5,7},{7,5}} | collective-permute-start | bytes 1572872 | tf_op jit(solution)/shard_map/ppermute | solution.py:600
  127.0 18.7 %copy-start = (f32[2,32,2048]{2,1,0:T(8,128)S(1)}, f32[2,32,2048]{2,1,0:T(8,128)}, u32[]{:S(2)}) copy-start(f32[2,32,2048]{2,1,0:T(8,128)} %get-tuple-element.56.early_ref) | copy-start | bytes 1572868
  127.0 18.7 %copy-start.1 = (f32[2,32,2048]{2,1,0:T(8,128)S(1)}, f32[2,32,2048]{2,1,0:T(8,128)}, u32[]{:S(2)}) copy-start(f32[2,32,2048]{2,1,0:T(8,128)} %get-tuple-element.55.base_ref) | copy-start | bytes 1572868
  127.0 18.7 %copy-start.2 = (f32[2,32,2048]{2,1,0:T(8,128)S(1)}, f32[2,32,2048]{2,1,0:T(8,128)}, u32[]{:S(2)}) copy-start(f32[2,32,2048]{2,1,0:T(8,128)} %get-tuple-element.57.own_ref) | copy-start | bytes 1572868
  145.9 35.6 %collective-permute-start.2 = (f32[4,32,2048]{2,1,0:T(8,128)S(1)}, f32[4,32,2048]{2,1,0:T(8,128)S(1)}, u32[]{:S(2)}, u32[]{:S(2)}) collective-permute-start(f32[4,32,2048]{2,1,0:T(8,128)S(1)} %last_sums.1.refs_0_), channel_id=1, source_target_pairs={{0,1},{1,0},{2,3},{3,2},{4,5},{5,4},{6,7},{7,6}} | collective-permute-start | bytes 3145736 | tf_op jit(solution)/shard_map/ppermute | solution.py:612
  146.0 35.4 %collective-permute-start.1 = (f32[4,32,2048]{2,1,0:T(8,128)S(1)}, f32[4,32,2048]{2,1,0:T(8,128)S(1)}, u32[]{:S(2)}, u32[]{:S(2)}) collective-permute-start(f32[4,32,2048]{2,1,0:T(8,128)S(1)} %last_sums.1.refs_0_), channel_id=1, source_target_pairs={{0,2},{2,0},{1,3},{3,1},{4,6},{6,4},{5,7},{7,5}} | collective-permute-start | bytes 3145736 | tf_op jit(solution)/shard_map/ppermute | solution.py:611
  181.4 2.7 %collective-permute-start.3 = (f32[4,32,2048]{2,1,0:T(8,128)S(1)}, f32[4,32,2048]{2,1,0:T(8,128)S(1)}, u32[]{:S(2)}, u32[]{:S(2)}) collective-permute-start(f32[4,32,2048]{2,1,0:T(8,128)S(1)} %collective-permute-done.1.refs_1_), channel_id=1, source_target_pairs={{0,1},{1,0},{2,3},{3,2},{4,5},{5,4},{6,7},{7,6}} | collective-permute-start | bytes 3145736 | tf_op jit(solution)/shard_map/ppermute | solution.py:615
